TPU v7x, 32 devices: a whole 2x2x4 slice. The times are simulated.
32 devices in a mesh: dp: 2 (over x), tp: 4 (over z), cp: 4 (over y, core).
Axes of the slice: x: 2, y: 2, z: 4, core: 2. Of those that a mesh axis runs over, the one named last changes fastest.
Arguments:
- x_tokens: bfloat16 [24576, 2048], P(('dp', 'cp', 'tp')), parts along dimension 0
- w_q: bfloat16 [2048, 24, 128], P(None, 'tp')
- w_k: bfloat16 [2048, 24, 128], P(None, 'tp')
- w_v: bfloat16 [2048, 24, 128], P(None, 'tp')
- w_o: bfloat16 [24, 128, 2048], P('tp')
Outputs:
- output: bfloat16 [24576, 2048], P(('dp', 'cp', 'tp')), parts along dimension 0
There are 2 independent parts. A program takes and returns all parts, laid end to end along the dimension named above; an argument that names none is the same for every part.
All inputs are finite; a program needn't handle non-finite values.
Results may differ from a plain program's by a relative error of at most 0.00553008.
Values are sent between devices in bfloat16 or wider.
A program may use at most 1 GiB of HBM per device.

v0:
```python
import jax
import jax.numpy as jnp
from jax import lax
from jax.sharding import PartitionSpec as P

NEG_BIG = -1e30


def online_update(q_blk, k_blk, v_blk, softmax_state, causal_mask):
    row_max, row_sum, out_acc = softmax_state
    inv_sqrt = q_blk.shape[-1] ** -0.5
    scores = jnp.einsum('qhe,khe->hqk', q_blk, k_blk, preferred_element_type=jnp.float32) * inv_sqrt
    if causal_mask is not None:
        scores = jnp.where(causal_mask, scores, NEG_BIG)
    new_max = jnp.maximum(row_max, scores.max(axis=-1))
    rescale = jnp.exp(row_max - new_max)
    weights = jnp.exp(scores - new_max[..., None])
    new_sum = rescale * row_sum + weights.sum(axis=-1)
    new_acc = rescale[..., None] * out_acc + jnp.einsum('hqk,khe->hqe', weights.astype(jnp.bfloat16), v_blk, preferred_element_type=jnp.float32)
    return new_max, new_sum, new_acc


def empty_state(n_heads, n_rows, head_dim):
    return (jnp.full((n_heads, n_rows), NEG_BIG, jnp.float32), jnp.zeros((n_heads, n_rows), jnp.float32), jnp.zeros((n_heads, n_rows, head_dim), jnp.float32))


def solution(mesh):
    cp_size = mesh.shape['cp']
    send_perm = [(rank_from, (rank_from + 1) % cp_size) for rank_from in range(cp_size)]

    def device_fn(x_loc, w_q, w_k, w_v, w_o):
        x_shard = lax.all_gather(x_loc, 'tp', axis=0, tiled=True)
        shard_len = x_shard.shape[0]
        block_len = shard_len // 2
        n_heads = w_q.shape[1]
        head_dim = w_q.shape[2]

        def project(weight):
            return jnp.einsum('sd,dhe->she', x_shard, weight, preferred_element_type=jnp.float32).astype(jnp.bfloat16)

        q_all = project(w_q)
        k_all = project(w_k)
        v_all = project(w_v)
        my_rank = lax.axis_index('cp')
        row_ids = lax.broadcasted_iota(jnp.int32, (block_len, shard_len), 0)
        col_ids = lax.broadcasted_iota(jnp.int32, (block_len, shard_len), 1)
        lo_mask = col_ids[:, :block_len] <= row_ids[:, :block_len]
        hi_mask = col_ids <= row_ids + block_len
        lo_state = online_update(q_all[:block_len], k_all[:block_len], v_all[:block_len], empty_state(n_heads, block_len, head_dim), lo_mask)
        hi_state = online_update(q_all[block_len:], k_all, v_all, empty_state(n_heads, block_len, head_dim), hi_mask)
        start_state = tuple(jnp.concatenate([lo_part, hi_part], axis=1) for lo_part, hi_part in zip(lo_state, hi_state))

        def keys_before(operands):
            k_blk, v_blk, softmax_state = operands
            return online_update(q_all, k_blk[:block_len], v_blk[:block_len], softmax_state, None)

        def keys_after(operands):
            k_blk, v_blk, softmax_state = operands
            upper_state = tuple(piece[:, block_len:] for piece in softmax_state)
            updated = online_update(q_all[block_len:], k_blk, v_blk, upper_state, None)
            return tuple(jnp.concatenate([piece[:, :block_len], fresh], axis=1) for piece, fresh in zip(softmax_state, updated))

        def kv_step(step_idx, loop_carry):
            k_cur, v_cur, softmax_state = loop_carry
            k_cur, v_cur = lax.ppermute((k_cur, v_cur), 'cp', send_perm)
            rank_from = (my_rank - step_idx) % cp_size
            softmax_state = lax.cond(rank_from < my_rank, keys_before, keys_after, (k_cur, v_cur, softmax_state))
            return k_cur, v_cur, softmax_state

        final_carry = lax.fori_loop(1, cp_size, kv_step, (k_all, v_all, start_state))
        final_state = final_carry[2]
        attn_out = (final_state[2] / final_state[1][..., None]).astype(jnp.bfloat16)
        y_part = jnp.einsum('hqe,hed->qd', attn_out, w_o, preferred_element_type=jnp.float32)
        y_loc = lax.psum_scatter(y_part, 'tp', scatter_dimension=0, tiled=True)
        return y_loc.astype(jnp.bfloat16)

    seq_spec = P(('dp', 'cp', 'tp'), None)
    head_spec = P(None, 'tp', None)
    return jax.shard_map(device_fn, mesh=mesh, in_specs=(seq_spec, head_spec, head_spec, head_spec, P('tp', None, None)), out_specs=seq_spec, check_vma=False)
```

profile of v0, /device:TPU:0, one launch (start us, length us, event | category | flops | bytes accessed | tf_op | source)
XLA Modules:
  0.0 1655.1 jit_solution(3127959830397754457)
XLA Ops:
  7.3 2.1 add_compare_fusion
  9.4 6.0 iota_compare_fusion
  15.4 215.0 %all-gather.2.cloned.1.call-done = bf16[3072,2048]{1,0:T(8,128)(2,1)} async-done(((bf16[768,2048]{1,0:T(8,128)(2,1)}), bf16[3072,2048]{1,0:T(8,128)(2,1)}) %all-gather.2.cloned.1.call-update) | async-done | bytes 12582928 | tf_op jit(solution)/shard_map/all_gather | solution.py:32
  230.4 16.1 fusion.43
  246.4 11.4 fusion.37
  257.9 23.6 %fusion.25 = (f32[6,1536]{1,0:T(8,128)S(1)}, f32[6,1536,1536]{1,2,0:T(8,128)}) fusion(pred[1536,1536]{0,1:T(8,128)(4,1)} %add_compare_fusion, bf16[3072,6,128]{2,0,1:T(8,128)(2,1)} %fusion.37, bf16[3072,6,128]{2,0,1:T(8,128)(2,1)} %fusion.43), kind=kOutput, calls=%fused_computation.36 | convolution fusion | flops 3666336768 | bytes 63737856 | tf_op jit(solution)/shard_map/qhe,khe->hqk/dot_general | solution.py:12
  281.5 42.8 %fusion.19 = (f32[6,1536]{1,0:T(8,128)S(1)}, f32[6,1536,3072]{2,1,0:T(8,128)}) fusion(pred[1536,3072]{1,0:T(8,128)(4,1)} %iota_compare_fusion, bf16[3072,6,128]{2,0,1:T(8,128)(2,1)} %fusion.37, bf16[3072,6,128]{2,0,1:T(8,128)(2,1)} %fusion.43), kind=kOutput, calls=%fused_computation.29 | convolution fusion | flops 7332682752 | bytes 125079552 | tf_op jit(solution)/shard_map/qhe,khe->hqk/dot_general | solution.py:12
  324.3 39.1 %fusion.21 = f32[6,1536]{1,0:T(8,128)S(1)} fusion(f32[6,1536,3072]{2,1,0:T(8,128)} %get-tuple-element.294, f32[6,1536]{1,0:T(8,128)S(1)} %get-tuple-element.297, pred[1536,3072]{1,0:T(8,128)(4,1)} %iota_compare_fusion), kind=kLoop, calls=%fused_computation.31 | loop fusion | flops 113236992 | bytes 118038528 | tf_op jit(solution)/shard_map/reduce_sum | solution.py:18
  364.1 19.3 %fusion.27 = f32[6,1536]{1,0:T(8,128)S(1)} fusion(f32[6,1536,1536]{1,2,0:T(8,128)} %get-tuple-element.296, f32[6,1536]{1,0:T(8,128)S(1)} %get-tuple-element.298, pred[1536,1536]{0,1:T(8,128)(4,1)} %add_compare_fusion), kind=kLoop, calls=%fused_computation.38 | loop fusion | flops 56613888 | bytes 59056128 | tf_op jit(solution)/shard_map/reduce_sum | solution.py:18
  384.0 15.3 fusion.40
  399.3 44.7 %fusion.47 = f32[6,1536,128]{2,1,0:T(8,128)} fusion(bf16[3072,6,128]{2,0,1:T(8,128)(2,1)} %fusion.40, f32[6,1536,3072]{2,1,0:T(8,128)} %get-tuple-element.294, f32[6,1536]{1,0:T(8,128)S(1)} %get-tuple-element.297, pred[1536,3072]{1,0:T(8,128)(4,1)} %iota_compare_fusion, f32[6,1536]{1,0:T(8,128)S(1)} %copy-done.3), kind=kOutput, calls=%fused_computation.56 | convolution fusion | flops 7362183168 | bytes 127475712 | tf_op jit(solution)/shard_map/hqk,khe->hqe/dot_general | solution.py:19
  444.0 26.2 %fusion.50 = f32[6,1536,128]{2,1,0:T(8,128)} fusion(f32[6,1536,1536]{1,2,0:T(8,128)} %get-tuple-element.296, f32[6,1536]{1,0:T(8,128)S(1)} %get-tuple-element.298, pred[1536,1536]{0,1:T(8,128)(4,1)} %add_compare_fusion, bf16[3072,6,128]{2,0,1:T(8,128)(2,1)} %fusion.40, f32[6,1536]{1,0:T(8,128)S(1)} %copy-done.4), kind=kOutput, calls=%fused_computation.57 | convolution fusion | flops 3681681408 | bytes 66134016 | tf_op jit(solution)/shard_map/hqk,khe->hqe/dot_general | solution.py:19
  470.1 7.9 pad_maximum_fusion.3
  478.1 737.6 %while.23 = (s32[]{:T(128)}, bf16[3072,6,128]{2,0,1:T(8,128)(2,1)}, bf16[3072,6,128]{2,0,1:T(8,128)(2,1)}, f32[6,3072]{1,0:T(8,128)S(1)}, f32[6,3072]{1,0:T(8,12...) while((s32[]{:T(128)}, bf16[3072,6,128]{2,0,1:T(8,128)(2,1)}, ...), condition=%wide.region_11.12_spmd, body=%wide.region_4.11_spmd.sunk | while | flops 14726780928 | bytes 447308288 | solution.py:70
  478.4 1.5 collective-permute-start
  479.9 52.0 %collective-permute-done.1 = bf16[3072,6,128]{2,0,1:T(8,128)(2,1)} collective-permute-done((bf16[3072,6,128]{2,0,1:T(8,128)(2,1)}, bf16[3072,6,128]{2,0,1:T(8,128)(2,1)}, u32[]{:S(2)}, u32[]{:S(2)}) %collective-permute-start.1) | collective-permute-done | bytes 4718624 | tf_op jit(solution)/shard_map/while/body/eval_jaxpr/ppermute | solution.py:65
  531.9 50.6 %collective-permute-done = bf16[3072,6,128]{2,0,1:T(8,128)(2,1)} collective-permute-done((bf16[3072,6,128]{2,0,1:T(8,128)(2,1)}, bf16[3072,6,128]{2,0,1:T(8,128)(2,1)}, u32[]{:S(2)}, u32[]{:S(2)}) %collective-permute-start) | collective-permute-done | bytes 4718624 | tf_op jit(solution)/shard_map/while/body/eval_jaxpr/ppermute | solution.py:65
  582.4 131.3 %conditional.2 = (f32[6,3072]{1,0:T(8,128)}, f32[6,3072]{1,0:T(8,128)S(1)}, f32[6,3072,128]{2,1,0:T(8,128)}) conditional(s32[]{:T(128)} %convert_element_type.67, (f32[6,3072]{1,0:T(8,128)S(1)}, bf16[3072,6,128]{2,0,1:T(8,128)(2,1)}, bf16[3072,6,128]{2,0,1:T(8,128)(2,1)}, f32[6,3072]{1,0:T(8,128)S(1)}, f32[6,3072,128]{2,1,0:T(8,128)}, ...), branch_computations={%region_5.7_spmd, %region_8.10_spmd} | conditional | flops 14726780928 | bytes 390537312 | solution.py:67
  582.4 4.8 slice.35
  587.2 40.3 %multiply_reduce_fusion = (f32[6,1536]{1,0:T(8,128)S(1)}, f32[6,1536,3072]{2,1,0:T(8,128)}) fusion(bf16[3072,6,128]{2,0,1:T(8,128)(2,1)} %get-tuple-element.235, bf16[3072,6,128]{2,0,1:T(8,128)(2,1)} %get-tuple-element.234), kind=kOutput, calls=%fused_computation.1 | convolution fusion | flops 7304371200 | bytes 120360960 | tf_op jit(solution)/shard_map/while/body/eval_jaxpr/cond/branch_0_fun/qhe,khe->hqk/dot_general | solution.py:12
  627.6 34.8 %fusion.1 = f32[6,1536]{1,0:T(8,128)S(1)} fusion(f32[6,1536,3072]{2,1,0:T(8,128)} %get-tuple-element.284, f32[6,1536]{1,0:T(8,128)S(1)} %slice_maximum_fusion), kind=kLoop, calls=%fused_computation.3 | loop fusion | flops 84925440 | bytes 113319936 | tf_op jit(solution)/shard_map/while/body/eval_jaxpr/cond/branch_0_fun/reduce_sum | solution.py:18
  663.1 42.0 %multiply_add_fusion = f32[6,1536,128]{2,1,0:T(8,128)} fusion(f32[6,3072,128]{2,1,0:T(8,128)} %get-tuple-element.237, bf16[3072,6,128]{2,0,1:T(8,128)(2,1)} %get-tuple-element.238, f32[6,1536,3072]{2,1,0:T(8,128)} %get-tuple-element.284, f32[6,1536]{1,0:T(8,128)S(1)} %slice_maximum_fusion, f32[6,1536]{1,0:T(8,128)S(1)} %get-tuple-element.278), kind=kOutput, calls=%fused_computation.6 | convolution fusion | flops 7335051264 | bytes 127475712 | tf_op jit(solution)/shard_map/while/body/eval_jaxpr/cond/branch_0_fun/hqk,khe->hqe/dot_general | solution.py:19
  705.1 7.9 pad_maximum_fusion
  714.6 4.7 copy.30
  719.3 4.8 copy.29
  724.1 53.5 %collective-permute-done.1 = bf16[3072,6,128]{2,0,1:T(8,128)(2,1)} collective-permute-done((bf16[3072,6,128]{2,0,1:T(8,128)(2,1)}, bf16[3072,6,128]{2,0,1:T(8,128)(2,1)}, u32[]{:S(2)}, u32[]{:S(2)}) %collective-permute-start.1) | collective-permute-done | bytes 4718624 | tf_op jit(solution)/shard_map/while/body/eval_jaxpr/ppermute | solution.py:65
  777.7 50.6 %collective-permute-done = bf16[3072,6,128]{2,0,1:T(8,128)(2,1)} collective-permute-done((bf16[3072,6,128]{2,0,1:T(8,128)(2,1)}, bf16[3072,6,128]{2,0,1:T(8,128)(2,1)}, u32[]{:S(2)}, u32[]{:S(2)}) %collective-permute-start) | collective-permute-done | bytes 4718624 | tf_op jit(solution)/shard_map/while/body/eval_jaxpr/ppermute | solution.py:65
  828.2 131.3 %conditional.2 = (f32[6,3072]{1,0:T(8,128)}, f32[6,3072]{1,0:T(8,128)S(1)}, f32[6,3072,128]{2,1,0:T(8,128)}) conditional(s32[]{:T(128)} %convert_element_type.67, (f32[6,3072]{1,0:T(8,128)S(1)}, bf16[3072,6,128]{2,0,1:T(8,128)(2,1)}, bf16[3072,6,128]{2,0,1:T(8,128)(2,1)}, f32[6,3072]{1,0:T(8,128)S(1)}, f32[6,3072,128]{2,1,0:T(8,128)}, ...), branch_computations={%region_5.7_spmd, %region_8.10_spmd} | conditional | flops 14726780928 | bytes 390537312 | solution.py:67
  828.2 4.8 slice.35
  833.0 40.3 %multiply_reduce_fusion = (f32[6,1536]{1,0:T(8,128)S(1)}, f32[6,1536,3072]{2,1,0:T(8,128)}) fusion(bf16[3072,6,128]{2,0,1:T(8,128)(2,1)} %get-tuple-element.235, bf16[3072,6,128]{2,0,1:T(8,128)(2,1)} %get-tuple-element.234), kind=kOutput, calls=%fused_computation.1 | convolution fusion | flops 7304371200 | bytes 120360960 | tf_op jit(solution)/shard_map/while/body/eval_jaxpr/cond/branch_0_fun/qhe,khe->hqk/dot_general | solution.py:12
  873.3 34.8 %fusion.1 = f32[6,1536]{1,0:T(8,128)S(1)} fusion(f32[6,1536,3072]{2,1,0:T(8,128)} %get-tuple-element.284, f32[6,1536]{1,0:T(8,128)S(1)} %slice_maximum_fusion), kind=kLoop, calls=%fused_computation.3 | loop fusion | flops 84925440 | bytes 113319936 | tf_op jit(solution)/shard_map/while/body/eval_jaxpr/cond/branch_0_fun/reduce_sum | solution.py:18
  908.8 42.0 %multiply_add_fusion = f32[6,1536,128]{2,1,0:T(8,128)} fusion(f32[6,3072,128]{2,1,0:T(8,128)} %get-tuple-element.237, bf16[3072,6,128]{2,0,1:T(8,128)(2,1)} %get-tuple-element.238, f32[6,1536,3072]{2,1,0:T(8,128)} %get-tuple-element.284, f32[6,1536]{1,0:T(8,128)S(1)} %slice_maximum_fusion, f32[6,1536]{1,0:T(8,128)S(1)} %get-tuple-element.278), kind=kOutput, calls=%fused_computation.6 | convolution fusion | flops 7335051264 | bytes 127475712 | tf_op jit(solution)/shard_map/while/body/eval_jaxpr/cond/branch_0_fun/hqk,khe->hqe/dot_general | solution.py:19
  950.9 7.9 pad_maximum_fusion
  960.4 4.7 copy.30
  965.1 4.8 copy.29
  969.9 53.5 %collective-permute-done.1 = bf16[3072,6,128]{2,0,1:T(8,128)(2,1)} collective-permute-done((bf16[3072,6,128]{2,0,1:T(8,128)(2,1)}, bf16[3072,6,128]{2,0,1:T(8,128)(2,1)}, u32[]{:S(2)}, u32[]{:S(2)}) %collective-permute-start.1) | collective-permute-done | bytes 4718624 | tf_op jit(solution)/shard_map/while/body/eval_jaxpr/ppermute | solution.py:65
  1023.4 50.6 %collective-permute-done = bf16[3072,6,128]{2,0,1:T(8,128)(2,1)} collective-permute-done((bf16[3072,6,128]{2,0,1:T(8,128)(2,1)}, bf16[3072,6,128]{2,0,1:T(8,128)(2,1)}, u32[]{:S(2)}, u32[]{:S(2)}) %collective-permute-start) | collective-permute-done | bytes 4718624 | tf_op jit(solution)/shard_map/while/body/eval_jaxpr/ppermute | solution.py:65
  1074.0 131.3 %conditional.2 = (f32[6,3072]{1,0:T(8,128)}, f32[6,3072]{1,0:T(8,128)S(1)}, f32[6,3072,128]{2,1,0:T(8,128)}) conditional(s32[]{:T(128)} %convert_element_type.67, (f32[6,3072]{1,0:T(8,128)S(1)}, bf16[3072,6,128]{2,0,1:T(8,128)(2,1)}, bf16[3072,6,128]{2,0,1:T(8,128)(2,1)}, f32[6,3072]{1,0:T(8,128)S(1)}, f32[6,3072,128]{2,1,0:T(8,128)}, ...), branch_computations={%region_5.7_spmd, %region_8.10_spmd} | conditional | flops 14726780928 | bytes 390537312 | solution.py:67
  1074.0 4.8 slice.35
  1078.8 40.3 %multiply_reduce_fusion = (f32[6,1536]{1,0:T(8,128)S(1)}, f32[6,1536,3072]{2,1,0:T(8,128)}) fusion(bf16[3072,6,128]{2,0,1:T(8,128)(2,1)} %get-tuple-element.235, bf16[3072,6,128]{2,0,1:T(8,128)(2,1)} %get-tuple-element.234), kind=kOutput, calls=%fused_computation.1 | convolution fusion | flops 7304371200 | bytes 120360960 | tf_op jit(solution)/shard_map/while/body/eval_jaxpr/cond/branch_0_fun/qhe,khe->hqk/dot_general | solution.py:12
  1119.1 34.8 %fusion.1 = f32[6,1536]{1,0:T(8,128)S(1)} fusion(f32[6,1536,3072]{2,1,0:T(8,128)} %get-tuple-element.284, f32[6,1536]{1,0:T(8,128)S(1)} %slice_maximum_fusion), kind=kLoop, calls=%fused_computation.3 | loop fusion | flops 84925440 | bytes 113319936 | tf_op jit(solution)/shard_map/while/body/eval_jaxpr/cond/branch_0_fun/reduce_sum | solution.py:18
  1154.6 42.0 %multiply_add_fusion = f32[6,1536,128]{2,1,0:T(8,128)} fusion(f32[6,3072,128]{2,1,0:T(8,128)} %get-tuple-element.237, bf16[3072,6,128]{2,0,1:T(8,128)(2,1)} %get-tuple-element.238, f32[6,1536,3072]{2,1,0:T(8,128)} %get-tuple-element.284, f32[6,1536]{1,0:T(8,128)S(1)} %slice_maximum_fusion, f32[6,1536]{1,0:T(8,128)S(1)} %get-tuple-element.278), kind=kOutput, calls=%fused_computation.6 | convolution fusion | flops 7335051264 | bytes 127475712 | tf_op jit(solution)/shard_map/while/body/eval_jaxpr/cond/branch_0_fun/hqk,khe->hqe/dot_general | solution.py:19
  1196.7 7.9 pad_maximum_fusion
  1206.2 4.7 copy.30
  1210.9 4.8 copy.29
  1215.7 16.1 convolution_bitcast_fusion
  1231.8 411.3 %reduce-scatter.2.cloned.1.call-done = f32[768,2048]{1,0:T(8,128)} async-done(((f32[3072,2048]{1,0:T(8,128)}), f32[768,2048]{1,0:T(8,128)}) %reduce-scatter.2.cloned.1.call-update) | async-done | bytes 6291472 | tf_op jit(solution)/shard_map/reduce_scatter | solution.py:74
  1643.1 4.9 convert_element_type.43
  (49 shorter events, 8.9 us)
Async XLA Ops:
  6.5 1209.1 %copy-start = (bf16[6,128,2048]{2,1,0:T(8,128)(2,1)S(1)}, bf16[6,128,2048]{2,1,0:T(8,128)(2,1)}, u32[]{:S(2)}) copy-start(bf16[6,128,2048]{2,1,0:T(8,128)(2,1)} %param.13) | copy-start | bytes 9437188
  6.5 223.8 %all-gather.2.cloned.1.call-start = ((), (), s32[]{:S(2)}) async-start(), calls=%async_computation.1 | async-start | bytes 15728640 | tf_op jit(solution)/shard_map/all_gather | solution.py:32
  7.3 1635.8 %reduce-scatter.2.cloned.1.call-start = ((), (), s32[]{:S(2)}) async-start(), calls=%async_computation.2 | async-start | bytes 31457280 | tf_op jit(solution)/shard_map/reduce_scatter | solution.py:74
  230.4 16.1 copy-start.5
  230.4 16.1 copy-start.6
  384.0 15.3 copy-start.3
  399.3 44.7 %copy-start.4 = (f32[6,1536]{1,0:T(8,128)S(1)}, f32[6,1536]{1,0:T(8,128)}, u32[]{:S(2)}) copy-start(f32[6,1536]{1,0:T(8,128)} %get-tuple-element.289) | copy-start | bytes 110596
  478.3 53.6 %collective-permute-start.1 = (bf16[3072,6,128]{2,0,1:T(8,128)(2,1)}, bf16[3072,6,128]{2,0,1:T(8,128)(2,1)}, u32[]{:S(2)}, u32[]{:S(2)}) collective-permute-start(bf16[3072,6,128]{2,0,1:T(8,128)(2,1)} %get-tuple-element.374), channel_id=1, source_target_pairs={{0,1},{1,2},{2,3},{3,0},{4,5},{5,6},{6,7},{7,4},{8,9},{9,10},{10,1... | collective-permute-start | bytes 14155784 | tf_op jit(solution)/shard_map/while/body/eval_jaxpr/ppermute | solution.py:65
  478.4 104.0 %collective-permute-start = (bf16[3072,6,128]{2,0,1:T(8,128)(2,1)}, bf16[3072,6,128]{2,0,1:T(8,128)(2,1)}, u32[]{:S(2)}, u32[]{:S(2)}) collective-permute-start(bf16[3072,6,128]{2,0,1:T(8,128)(2,1)} %get-tuple-element.373), channel_id=1, source_target_pairs={{0,1},{1,2},{2,3},{3,0},{4,5},{5,6},{6,7},{7,4},{8,9},{9,10},{10,1... | collective-permute-start | bytes 14155784 | tf_op jit(solution)/shard_map/while/body/eval_jaxpr/ppermute | solution.py:65
  705.1 7.9 copy-start.1
  705.1 7.9 copy-start.2
  724.1 53.5 %collective-permute-start.1 = (bf16[3072,6,128]{2,0,1:T(8,128)(2,1)}, bf16[3072,6,128]{2,0,1:T(8,128)(2,1)}, u32[]{:S(2)}, u32[]{:S(2)}) collective-permute-start(bf16[3072,6,128]{2,0,1:T(8,128)(2,1)} %get-tuple-element.374), channel_id=1, source_target_pairs={{0,1},{1,2},{2,3},{3,0},{4,5},{5,6},{6,7},{7,4},{8,9},{9,10},{10,1... | collective-permute-start | bytes 14155784 | tf_op jit(solution)/shard_map/while/body/eval_jaxpr/ppermute | solution.py:65
  724.1 104.1 %collective-permute-start = (bf16[3072,6,128]{2,0,1:T(8,128)(2,1)}, bf16[3072,6,128]{2,0,1:T(8,128)(2,1)}, u32[]{:S(2)}, u32[]{:S(2)}) collective-permute-start(bf16[3072,6,128]{2,0,1:T(8,128)(2,1)} %get-tuple-element.373), channel_id=1, source_target_pairs={{0,1},{1,2},{2,3},{3,0},{4,5},{5,6},{6,7},{7,4},{8,9},{9,10},{10,1... | collective-permute-start | bytes 14155784 | tf_op jit(solution)/shard_map/while/body/eval_jaxpr/ppermute | solution.py:65
  950.9 7.9 copy-start.1
  950.9 7.9 copy-start.2
  969.9 53.5 %collective-permute-start.1 = (bf16[3072,6,128]{2,0,1:T(8,128)(2,1)}, bf16[3072,6,128]{2,0,1:T(8,128)(2,1)}, u32[]{:S(2)}, u32[]{:S(2)}) collective-permute-start(bf16[3072,6,128]{2,0,1:T(8,128)(2,1)} %get-tuple-element.374), channel_id=1, source_target_pairs={{0,1},{1,2},{2,3},{3,0},{4,5},{5,6},{6,7},{7,4},{8,9},{9,10},{10,1... | collective-permute-start | bytes 14155784 | tf_op jit(solution)/shard_map/while/body/eval_jaxpr/ppermute | solution.py:65
  969.9 104.1 %collective-permute-start = (bf16[3072,6,128]{2,0,1:T(8,128)(2,1)}, bf16[3072,6,128]{2,0,1:T(8,128)(2,1)}, u32[]{:S(2)}, u32[]{:S(2)}) collective-permute-start(bf16[3072,6,128]{2,0,1:T(8,128)(2,1)} %get-tuple-element.373), channel_id=1, source_target_pairs={{0,1},{1,2},{2,3},{3,0},{4,5},{5,6},{6,7},{7,4},{8,9},{9,10},{10,1... | collective-permute-start | bytes 14155784 | tf_op jit(solution)/shard_map/while/body/eval_jaxpr/ppermute | solution.py:65
  1196.7 7.9 copy-start.1
  1196.7 7.9 copy-start.2
Sparse Core Ops, SparseCore 0:
  8.9 221.4 all-gather.1
  1231.9 411.1 reduce-scatter.1
where the time goes:
time: 1660 us
  waiting for transfers between devices  938 us (57%)
  matrix products  443 us (27%)
  other arithmetic  213 us (13%)
  local copies, waits for them, and re-layouts  45.6 us (3%)
    reduce_scatter x1, waiting for transfers between devices, device_fn(): y_loc = lax.psum_scatter(y_part, 'tp', scatter_dimension=0, tiled=True)  411 us
    ppermute x6, waiting for transfers between devices, kv_step(): k_cur, v_cur = lax.ppermute((k_cur, v_cur), 'cp', send_perm)  311 us
    all_gather x1, waiting for transfers between devices, device_fn(): x_shard = lax.all_gather(x_loc, 'tp', axis=0, tiled=True)  215 us
    dot_general x5, matrix products, online_update(): jnp.einsum('hqk,khe->hqe', weights.astype(jnp.bfloat16), v_blk, preferred...  197 us
    dot_general x5, matrix products, online_update(): jnp.einsum('qhe,khe->hqk', q_blk, k_blk, preferred_element_type=jnp.float32)  187 us
    reduce_sum x5, other arithmetic, online_update(): new_sum = rescale * row_sum + weights.sum(axis=-1)  163 us
    dot_general x3, matrix products, project(): jnp.einsum('sd,dhe->she', x_shard, weight, preferred_element_type=jnp.flo...  42.8 us
  transfers between devices with their start and end apart: 8, of which 8 were waited for; matrix products, arithmetic and copies ran while one was open for 0% of the time, Pallas kernels for 0%

commit v1 on v0

v1 whole, which is shorter than its diff:
```python
import functools

import jax
import jax.numpy as jnp
import numpy as np
from jax import lax
from jax.experimental import pallas as pl
from jax.experimental.pallas import tpu as pltpu
from jax.sharding import PartitionSpec as P


LOG2E = 1.4426950408889634
ARRIVAL = ((0, 1, 2, 3), (1, 0, 2, 3), (2, 3, 1, 0), (3, 2, 1, 0))
HALF = 384
GROUPS = 3


def sub_block(run, rank, n_cp):
    if run < 2:
        return 2 * rank + run
    return 2 * (2 * n_cp - 1 - rank) + run - 2


LOCAL, REMOTE = (0, 1), (2, 3)


def key_slots(spec):
    return [4 * step + src for step, sources in spec for src in sources]


AVAIL = [
    key_slots([(0, LOCAL), (0, REMOTE), (1, LOCAL)]),
    key_slots([(0, LOCAL + REMOTE), (1, LOCAL + REMOTE), (2, LOCAL)]),
    key_slots([(0, LOCAL + REMOTE), (1, LOCAL + REMOTE), (2, LOCAL + REMOTE), (3, LOCAL)]),
    key_slots([(s, LOCAL + REMOTE) for s in range(4)]),
]
Q_SLOTS = [2, 3, 4, 4]
ROW = 20


def work_tables(n_tp, n_cp):
    def make(before, after):
        out = np.zeros((n_tp, n_cp, 5, ROW), np.int32)
        for z in range(n_tp):
            for r in range(n_cp):
                for i in range(Q_SLOTS[after]):
                    mine = sub_block(ARRIVAL[z][i], r, n_cp)
                    done = before >= 0 and i < Q_SLOTS[before]
                    keys = []
                    for j in AVAIL[after]:
                        if done and j in AVAIL[before]:
                            continue
                        other = sub_block(ARRIVAL[z][j // 4], r ^ (j % 4), n_cp)
                        if other < mine:
                            keys.append(j)
                    out[z, r, i, 0] = len(keys)
                    out[z, r, i, 1:1 + len(keys)] = keys
                order = (0, 1, 3, 2) if z in (1, 2) else (0, 1, 2, 3)
                out[z, r, 4, :4] = order
        return out.reshape(n_tp * n_cp, 5 * ROW)

    return make


def attend_kernel(cfg, tbl, *refs):
    (n_q, n_state, keys, final, rows, scale) = cfg
    refs = list(refs)
    q_in = [refs.pop(0) for _ in range(n_q)]
    kv_in = [refs.pop(0) for _ in keys]
    st_in = [[refs.pop(0) for _ in range(3)] for _ in range(n_state)]
    if final:
        o_out = [refs.pop(0) for _ in range(4)]
    else:
        st_out = [[refs.pop(0) for _ in range(3)] for _ in range(n_q)]
    q_scr, k_scr, v_scr, acc, m_scr, l_scr = refs
    hd = q_scr.shape[-1]

    def at(n):
        return pl.ds(n * rows, rows)

    for i in range(n_q):
        q_scr[at(i), :] = q_in[i][...]
    for j, ref in zip(keys, kv_in):
        k_scr[at(j), :] = ref[:, :hd]
        v_scr[at(j), :] = ref[:, hd:]
    for i in range(n_state):
        for dst, src in zip((acc, m_scr, l_scr), st_in[i]):
            dst[at(i), :] = src[...]

    def scores(q, kj, n):
        return lax.dot_general(q, k_scr[pl.ds(kj, n), :], (((1,), (1,)), ((), ())), preferred_element_type=jnp.float32)

    def lane_sums(p):
        out = p[:, :hd]
        for t in range(1, p.shape[1] // hd):
            out = out + p[:, t * hd:(t + 1) * hd]
        return out

    chunks = list(range(0, rows, HALF))

    for i in range(n_state, n_q):
        base = i * rows
        raws = [scores(q_scr[pl.ds(base + c, HALF), :], 4 * i * rows, c + HALF) for c in chunks]
        for c, s in zip(chunks, raws):
            n = c + HALF
            keep = lax.broadcasted_iota(jnp.int32, (HALF, n), 1) <= lax.broadcasted_iota(jnp.int32, (HALF, n), 0) + c
            s = jnp.where(keep, s * scale, -jnp.inf)
            m_new = jnp.broadcast_to(jnp.max(s, axis=1, keepdims=True), (HALF, hd))
            p = jnp.exp2(s - m_new[:, :1])
            here = pl.ds(base + c, HALF)
            l_scr[here, :] = lane_sums(p)
            m_scr[here, :] = m_new
            acc[here, :] = jnp.dot(p.astype(jnp.bfloat16), v_scr[pl.ds(4 * i * rows, n), :], preferred_element_type=jnp.float32)

    def update(base, kjs):
        def raw(c):
            q = q_scr[pl.ds(base + c, HALF), :]
            return [scores(q, kj, rows) for kj in kjs]

        nxt = raw(0)
        for n, c in enumerate(chunks):
            cur = nxt
            if n + 1 < len(chunks):
                nxt = raw(chunks[n + 1])
            here = pl.ds(base + c, HALF)
            m_old = m_scr[here, :]
            top = functools.reduce(jnp.maximum, cur)
            m_new = jnp.maximum(m_old, jnp.max(top, axis=1, keepdims=True) * scale)
            alpha = jnp.exp2(m_old - m_new)
            ps = [jnp.exp2(s * scale - m_new[:, :1]) for s in cur]
            sums = functools.reduce(jnp.add, [lane_sums(p) for p in ps])
            l_scr[here, :] = alpha * l_scr[here, :] + sums
            m_scr[here, :] = m_new
            pv = functools.reduce(jnp.add, [jnp.dot(p.astype(jnp.bfloat16), v_scr[pl.ds(kj, rows), :], preferred_element_type=jnp.float32) for p, kj in zip(ps, kjs)])
            acc[here, :] = alpha * acc[here, :] + pv

    def slot(i, _):
        base = pl.multiple_of(i * rows, rows)
        count = tbl[i * ROW]

        def key(n):
            return pl.multiple_of(tbl[i * ROW + 1 + n] * rows, rows)

        def two(n, _):
            update(base, [key(2 * n), key(2 * n + 1)])
            return 0

        lax.fori_loop(0, count // 2, two, 0)

        @pl.when(count % 2 == 1)
        def _():
            update(base, [key(count - 1)])

        return 0

    lax.fori_loop(0, n_q, slot, 0)

    if final:
        for j in range(4):
            here = pl.ds(pl.multiple_of(tbl[4 * ROW + j] * rows, rows), rows)
            total = jnp.sum(l_scr[here, :], axis=1, keepdims=True)
            o_out[j][...] = (acc[here, :] / total).astype(jnp.bfloat16)
    else:
        for i in range(n_q):
            for dst, src in zip(st_out[i], (acc, m_scr, l_scr)):
                dst[...] = src[at(i), :]


def attend(tbl, q_in, kv_in, keys, state, state_start, heads, final, hd, flops):
    first, count = heads
    rows = q_in[0].shape[0]
    n_q, n_state = len(q_in), len(state)
    scale = LOG2E * hd ** -0.5
    cfg = (n_q, n_state, tuple(keys), final, rows, scale)

    def spec(width, start):
        return pl.BlockSpec((rows, width), lambda h, t: (0, h + first - start))

    in_specs = [spec(hd, 0) for _ in q_in]
    in_specs += [spec(2 * hd, start) for _, start in kv_in]
    flat = [a for slot in state for a in slot]
    in_specs += [spec(hd, state_start) for _ in flat]
    if final:
        out_shape = [jax.ShapeDtypeStruct((rows, count * hd), jnp.bfloat16)] * 4
        out_specs = [pl.BlockSpec((rows, hd), lambda h, t: (0, h))] * 4
    else:
        out_shape = [jax.ShapeDtypeStruct((rows, count * hd), jnp.float32)] * (3 * n_q)
        out_specs = [pl.BlockSpec((rows, hd), lambda h, t: (0, h))] * (3 * n_q)
    outs = pl.pallas_call(
        functools.partial(attend_kernel, cfg),
        grid_spec=pltpu.PrefetchScalarGridSpec(
            num_scalar_prefetch=1,
            grid=(count,),
            in_specs=in_specs,
            out_specs=out_specs,
            scratch_shapes=[
                pltpu.VMEM((n_q * rows, hd), jnp.bfloat16),
                pltpu.VMEM((16 * rows, hd), jnp.bfloat16),
                pltpu.VMEM((16 * rows, hd), jnp.bfloat16),
            ] + [pltpu.VMEM((n_q * rows, hd), jnp.float32)] * 3,
        ),
        out_shape=out_shape,
        compiler_params=pltpu.CompilerParams(vmem_limit_bytes=60 * 2 ** 20),
        cost_estimate=pl.CostEstimate(flops=flops, bytes_accessed=2 ** 20, transcendentals=0),
    )(tbl, *q_in, *[a for a, _ in kv_in], *flat)
    if final:
        return list(outs)
    return [tuple(outs[3 * i:3 * i + 3]) for i in range(n_q)]


def out_kernel(n_groups, n_parts, tbl, *refs):
    o_in = refs[:4 * n_groups]
    w_in = refs[4 * n_groups:4 * n_groups + n_parts]
    y_ref, o_scr, w_scr, sem = refs[4 * n_groups + n_parts:]
    width, cols = o_in[0].shape[1], w_scr.shape[-1]
    copies = [pltpu.make_async_copy(w_in[s], w_scr.at[s], sem.at[s]) for s in range(n_parts)]
    for copy in copies:
        copy.start()
    for g in range(n_groups):
        for j in range(4):
            start = (j * n_groups + g) * width
            o_scr[:, start:start + width] = o_in[g * 4 + j][...]
    half = o_scr.shape[0] // 2
    for s in range(n_parts):
        copies[s].wait()
        there = pl.ds(pl.multiple_of(tbl[s] * cols, cols), cols)

        def rows_of(n, _):
            here = pl.ds(pl.multiple_of(n * half, half), half)
            y_ref[here, there] = jnp.dot(o_scr[here, :], w_scr[s], preferred_element_type=jnp.float32).astype(y_ref.dtype)
            return 0

        lax.fori_loop(0, 2, rows_of, 0)


def project_out(tbl, o_groups, w_parts):
    rows, _ = o_groups[0][0].shape
    depth, cols = w_parts[0].shape
    n_parts = len(w_parts)
    flat = [a for group in o_groups for a in group]
    return pl.pallas_call(
        functools.partial(out_kernel, len(o_groups), n_parts),
        in_specs=[pl.BlockSpec(memory_space=pltpu.SMEM)]
        + [pl.BlockSpec(memory_space=pltpu.VMEM) for _ in flat]
        + [pl.BlockSpec(memory_space=pl.ANY) for _ in w_parts],
        out_specs=pl.BlockSpec(memory_space=pltpu.VMEM),
        scratch_shapes=[
            pltpu.VMEM((rows, depth), jnp.bfloat16),
            pltpu.VMEM((n_parts, depth, cols), jnp.bfloat16),
            pltpu.SemaphoreType.DMA((n_parts,)),
        ],
        out_shape=jax.ShapeDtypeStruct((rows, n_parts * cols), jnp.bfloat16),
        compiler_params=pltpu.CompilerParams(vmem_limit_bytes=60 * 2 ** 20),
        cost_estimate=pl.CostEstimate(flops=2 * rows * depth * cols * n_parts, bytes_accessed=2 ** 24, transcendentals=0),
    )(tbl, *flat, *w_parts)


def solution(mesh):
    n_tp, n_cp = mesh.shape['tp'], mesh.shape['cp']
    make = work_tables(n_tp, n_cp)
    plans = [make(-1, 0), make(0, 1), make(1, 2), make(2, 3), make(1, 3)]

    def flip(axis, bit):
        n = mesh.shape[axis]
        return [(i, i ^ bit) for i in range(n)]

    def device_fn(x_loc, w_q, w_k, w_v, w_o):
        z, r = lax.axis_index('tp'), lax.axis_index('cp')
        d_model, n_heads, hd = w_q.shape
        inner = n_heads * hd
        ends = (z == 0) | (z == n_tp - 1)
        tables = [lax.dynamic_index_in_dim(jnp.asarray(p), z * n_cp + r, 0, keepdims=False) for p in plans]

        near = lax.ppermute(x_loc, 'tp', flip('tp', 1))
        mid = lax.ppermute(x_loc, 'tp', [(1, 2), (2, 1)])
        mid_out = lax.ppermute(mid, 'tp', [(1, 0), (2, 3)])
        far_mid = lax.ppermute(near, 'tp', [(1, 2), (2, 1)])
        far_out = lax.ppermute(far_mid, 'tp', [(1, 0), (2, 3)])

        wq = w_q.reshape(d_model, inner)
        wkv = jnp.concatenate([w_k, w_v], axis=2).reshape(d_model, 2 * inner)

        def project(xs, w):
            return jnp.dot(xs, w, preferred_element_type=jnp.float32).astype(jnp.bfloat16)

        def spread(kv):
            core = lax.ppermute(kv, 'cp', flip('cp', 1))
            chip = lax.ppermute(kv, 'cp', flip('cp', 2))
            both = lax.ppermute(chip, 'cp', flip('cp', 1))
            return [kv, core, chip, both]

        per = n_heads // GROUPS

        def spans(g):
            return slice(g * per * 2 * hd, (g + 1) * per * 2 * hd)

        def tie(value, *after):
            return lax.optimization_barrier((value,) + after)[0]

        q_steps, kv_all = [], {}

        def take(step, xs):
            for src, kv in enumerate(spread(project(xs, wkv))):
                kv_all[4 * step + src] = (kv, 0)
            q_steps.append(project(xs, wq))

        def pick(group, avail):
            return [kv_all[j] if j < 12 else kv_last[group][j] for j in avail]

        take(0, x_loc)
        take(1, near)
        first = attend(tables[0], q_steps[:2], pick(0, AVAIL[0]), AVAIL[0], [], 0, (0, n_heads), False, hd, 10 ** 9)
        take(2, jnp.where(ends, tie(mid_out, first[0][2]), mid))

        second = [None] * GROUPS

        def attend_second(g, tbl):
            second[g] = attend(tbl, q_steps[:3], pick(0, AVAIL[1]), AVAIL[1], first, 0, (g * per, per), False, hd, 10 ** 9)

        for g in range(GROUPS - 1):
            attend_second(g, tables[1])
        x_last = jnp.where(ends, tie(far_out, *[s[0][2] for s in second[:-1]]), far_mid)
        kv_last, own_last = [], []
        for g in range(GROUPS):
            kv = project(x_last, wkv[:, spans(g)])
            own_last.append(kv)
            kv_last.append({12 + src: (a, g * per) for src, a in enumerate(spread(kv))})
        q_steps.append(project(x_last, wq))
        attend_second(GROUPS - 1, tie(tables[1], *own_last, q_steps[3]))

        o_groups = []
        after = second[-1][0][2]
        for g in range(GROUPS):
            heads = (g * per, per)
            o_send = attend(tie(tables[4], after), q_steps, pick(g, AVAIL[3]), AVAIL[3], second[g], g * per, heads, True, hd, 3 * 10 ** 10)
            after = o_send[0]
            o_groups.append([o_send[0]] + [lax.ppermute(o_send[j], 'tp', flip('tp', j)) for j in range(1, 4)])

        dp = lax.axis_index('dp')
        quarter = 2 * dp + lax.rem(r, 2)
        cols = d_model // 4
        w_part = lax.dynamic_slice(w_o.reshape(inner, d_model), (0, quarter * cols), (inner, cols))
        w_part = tie(w_part, own_last[-1])
        w_got = [lax.ppermute(w_part, 'tp', flip('tp', j)) for j in range(1, 4)]
        w_mine = jnp.concatenate([w_part] + [tie(w, o_groups[0][0]) for w in w_got], axis=0)
        w_x = lax.ppermute(w_mine, 'dp', flip('dp', 1))
        w_all = [w_mine, w_x, lax.ppermute(w_mine, 'cp', flip('cp', 1)), lax.ppermute(tie(w_x, o_groups[-1][0]), 'cp', flip('cp', 1))]
        out_tbl = jnp.stack([quarter, quarter ^ 2, quarter ^ 1, quarter ^ 3]).astype(jnp.int32)
        return project_out(out_tbl, o_groups, w_all)

    seq_spec = P(('dp', 'cp', 'tp'), None)
    head_spec = P(None, 'tp', None)

    return jax.shard_map(device_fn, mesh=mesh, in_specs=(seq_spec, head_spec, head_spec, head_spec, P('tp', None, None)), out_specs=seq_spec, check_vma=False)
```

time: 1660 us -> 648 us (0.39)
  the two profiles are of different devices: /device:TPU:0 before, /device:TPU:21 now
where the time goes in v1:
time: 648 us; the launch traced here: 644 us
  Pallas kernels  257 us (40%)
  waiting for transfers between devices  166 us (26%)
  starting transfers between devices  132 us (20%)
  matrix products  57.1 us (9%)
  local copies, waits for them, and re-layouts  25 us (4%)
  other arithmetic  7.13 us (1%)
    pallas_call x7, Pallas kernels, attend(): pl.pallas_call(functools.partial(attend_kernel, cfg), grid_spec=pltpu.Pre...  240 us
    ppermute x9, waiting for transfers between devices, device_fn(): lax.ppermute(o_send[j], 'tp', flip('tp', j))  97.3 us
    dot_general x10, matrix products, project(): jnp.dot(xs, w, preferred_element_type=jnp.float32).astype(jnp.bfloat16)  57.1 us
    ppermute x6, waiting for transfers between devices, spread(): chip = lax.ppermute(kv, 'cp', flip('cp', 2))  52.2 us
    ppermute x6, starting transfers between devices, spread(): both = lax.ppermute(chip, 'cp', flip('cp', 1))  44.9 us
    ppermute x3, starting transfers between devices, device_fn(): w_got = [lax.ppermute(w_part, 'tp', flip('tp', j)) for j in range(1, 4)]  38.4 us
    ppermute x6, starting transfers between devices, spread(): chip = lax.ppermute(kv, 'cp', flip('cp', 2))  22.3 us
    unnamed x38, local copies, waits for them, and re-layouts  19.2 us
  transfers between devices with their start and end apart: 38, of which 11 were waited for; matrix products, arithmetic and copies ran while one was open for 13% of the time, Pallas kernels for 37%

profile of v1, /device:TPU:21, one launch (start us, length us, event | category | flops | bytes accessed | tf_op | source)
XLA Modules:
  0.0 644.2 jit_solution(12534540056583151753)
XLA Ops:
  1.3 1.9 collective-permute-start.3
  3.2 4.7 copy.12
  7.9 4.6 copy.13
  12.6 4.1 pad_maximum_fusion
  16.7 6.3 fusion.refs_2_.refs_3_.refs_4_
  24.5 50.7 %collective-permute-done.6.refs_4_.refs_5_.refs_6_ = bf16[768,1536]{1,0:T(8,128)(2,1)} collective-permute-done((bf16[768,1536]{1,0:T(8,128)(2,1)}, bf16[768,1536]{1,0:T(8,128)(2,1)}, u32[]{:S(2)}, u32[]{:S(2)}) %collective-permute-start.6) | collective-permute-done | bytes 2359328 | tf_op jit(solution)/shard_map/ppermute | solution.py:288
  75.1 1.8 collective-permute-start.7
  77.0 4.2 collective-permute-start.4
  81.2 2.3 collective-permute-start.1
  83.6 8.3 %fusion.1.refs_6_.refs_7_.refs_8_ = bf16[768,1536]{1,0:T(8,128)(2,1)} fusion(bf16[2048,1536]{0,1:T(8,128)(2,1)S(1)} %bitcast.34, bf16[768,2048]{1,0:T(8,128)(2,1)} %collective-permute-done), kind=kOutput, calls=%fused_computation.7 | convolution fusion | flops 4833017856 | bytes 11796480 | tf_op jit(solution)/shard_map/dot_general | solution.py:284
  92.3 4.6 copy.11
  97.2 6.5 %convolution_convert_fusion.6.refs_0_ = bf16[768,768]{1,0:T(8,128)(2,1)} fusion(bf16[768,2048]{1,0:T(8,128)(2,1)} %param.8, bf16[2048,768]{0,1:T(8,128)(2,1)} %bitcast.41), kind=kOutput, calls=%fused_computation.17 | convolution fusion | flops 2416508928 | bytes 7471104 | tf_op jit(solution)/shard_map/dot_general | solution.py:284
  105.0 6.5 %convolution_convert_fusion.5.refs_1_ = bf16[768,768]{1,0:T(8,128)(2,1)} fusion(bf16[768,2048]{1,0:T(8,128)(2,1)} %collective-permute-done, bf16[2048,768]{0,1:T(8,128)(2,1)} %bitcast.42), kind=kOutput, calls=%fused_computation.16 | convolution fusion | flops 2416508928 | bytes 7471104 | tf_op jit(solution)/shard_map/dot_general | solution.py:284
  111.5 24.9 %shard_map.82 = (f32[768,768]{1,0:T(8,128)}, f32[768,768]{1,0:T(8,128)}, f32[768,768]{1,0:T(8,128)}, f32[768,768]{1,0:T(8,128)}, f32[768,768]{1,0:T(8,128)}, /*index=5*/f32[768,768]{1,0:T(8,128)}) custom-call(s32[100]{0:T(128)} %fusion.19.tbl, bf16[768,768]{1,0:T(8,128)(2,1)} %convolution_convert_fusion.6.refs_0_, ...), custom_call_target="tpu_custom_call" | custom-call | flops 1000000000 | bytes 1048576 | tf_op jit(solution)/shard_map/pallas_call | solution.py:189
  136.4 10.9 %collective-permute-done.4 = bf16[768,2048]{1,0:T(8,128)(2,1)} collective-permute-done((bf16[768,2048]{1,0:T(8,128)(2,1)}, bf16[768,2048]{1,0:T(8,128)(2,1)}, u32[]{:S(2)}, u32[]{:S(2)}) %collective-permute-start.4) | collective-permute-done | bytes 3145760 | tf_op jit(solution)/shard_map/ppermute | solution.py:276
  147.3 5.5 collective-permute-done.1
  152.8 3.5 collective-permute-start.2
  156.3 9.3 %convolution_convert_fusion.refs_11_.refs_12_ = bf16[768,1536]{1,0:T(8,128)(2,1)} fusion(bf16[2048,1536]{0,1:T(8,128)(2,1)} %bitcast.35, bf16[768,2048]{1,0:T(8,128)(2,1)} %collective-permute-done.4, bf16[768,2048]{1,0:T(8,128)(2,1)} %collective-permute-done.3, pred[]{:T(512)S(6)} %or.3), kind=kOutput, calls=%fused_computation.1 | convolution fusion | flops 4834590720 | bytes 14942209 | tf_op jit(solution)/shard_map/dot_general | solution.py:284
  165.6 5.1 collective-permute-start.12
  170.7 20.8 %collective-permute-start.10 = (bf16[768,1536]{1,0:T(8,128)(2,1)}, bf16[768,1536]{1,0:T(8,128)(2,1)}, u32[]{:S(2)}, u32[]{:S(2)}) collective-permute-start(bf16[768,1536]{1,0:T(8,128)(2,1)} %collective-permute-done.9.refs_9_.refs_10_), channel_id=1, source_target_pairs={{0,1},{1,0},{2,3},{3,2},{4,5},{5,4},{6,7},{7,6},{8,9},{9,8},{10,11... | collective-permute-start | bytes 7077896 | tf_op jit(solution)/shard_map/ppermute | solution.py:289
  194.0 6.6 %convolution_convert_fusion.4.refs_2_ = bf16[768,768]{1,0:T(8,128)(2,1)} fusion(bf16[2048,768]{0,1:T(8,128)(2,1)} %bitcast.43, bf16[768,2048]{1,0:T(8,128)(2,1)} %collective-permute-done.4, bf16[768,2048]{1,0:T(8,128)(2,1)} %collective-permute-done.3, pred[]{:T(512)S(6)} %or.3), kind=kOutput, calls=%fused_computation.15 | convolution fusion | flops 2418081792 | bytes 10616833 | tf_op jit(solution)/shard_map/dot_general | solution.py:284
  202.1 21.1 %collective-permute-start.13 = (bf16[768,1536]{1,0:T(8,128)(2,1)}, bf16[768,1536]{1,0:T(8,128)(2,1)}, u32[]{:S(2)}, u32[]{:S(2)}) collective-permute-start(bf16[768,1536]{1,0:T(8,128)(2,1)} %collective-permute-done.12.refs_14_), channel_id=1, source_target_pairs={{0,1},{1,0},{2,3},{3,2},{4,5},{5,4},{6,7},{7,6},{8,9},{9,8},{10,11... | collective-permute-start | bytes 7077896 | tf_op jit(solution)/shard_map/ppermute | solution.py:289
  223.2 19.3 %shard_map.84 = (f32[768,256]{1,0:T(8,128)}, f32[768,256]{1,0:T(8,128)}, f32[768,256]{1,0:T(8,128)}, f32[768,256]{1,0:T(8,128)}, f32[768,256]{1,0:T(8,128)}, /*i...) custom-call(s32[100]{0:T(128)} %fusion.18.tbl, ...), custom_call_target="tpu_custom_call" | custom-call | flops 1000000000 | bytes 1048576 | tf_op jit(solution)/shard_map/pallas_call | solution.py:189
  242.5 19.4 %shard_map.83 = (f32[768,256]{1,0:T(8,128)}, f32[768,256]{1,0:T(8,128)}, f32[768,256]{1,0:T(8,128)}, f32[768,256]{1,0:T(8,128)}, f32[768,256]{1,0:T(8,128)}, /*i...) custom-call(s32[100]{0:T(128)} %fusion.18.tbl, ...), custom_call_target="tpu_custom_call" | custom-call | flops 1000000000 | bytes 1048576 | tf_op jit(solution)/shard_map/pallas_call | solution.py:189
  261.9 2.4 broadcast_select_fusion
  264.3 4.5 fusion.8.refs_16_
  268.8 15.0 %collective-permute-start.15 = (bf16[768,512]{1,0:T(8,128)(2,1)}, bf16[768,512]{1,0:T(8,128)(2,1)}, u32[]{:S(2)}, u32[]{:S(2)}) collective-permute-start(bf16[768,512]{1,0:T(8,128)(2,1)} %fusion.8.refs_16_), channel_id=1, source_target_pairs={{0,2},{1,3},{2,0},{3,1},{4,6},{5,7},{6,4},{7,5},{8,10},{9,11},{10,... | collective-permute-start | bytes 2359304 | tf_op jit(solution)/shard_map/ppermute | solution.py:288
  283.8 2.7 fusion.14.refs_16_
  286.5 14.3 %collective-permute-start.34 = (bf16[768,512]{1,0:T(8,128)(2,1)S(1)}, bf16[768,512]{1,0:T(8,128)(2,1)}, u32[]{:S(2)}, u32[]{:S(2)}) collective-permute-start(bf16[768,512]{1,0:T(8,128)(2,1)S(1)} %constant_dynamic-slice_fusion), channel_id=1, source_target_pairs={{0,12},{4,8},{8,4},{12,0},{1,13},{5,9},{9,5},{13,1},{2,14},{6,10},... | collective-permute-start | bytes 2359304 | tf_op jit(solution)/shard_map/ppermute | solution.py:344
  300.8 2.7 fusion.11.refs_16_
  305.8 3.7 convolution_convert_fusion.3.refs_3_
  309.5 19.5 %shard_map.85 = (f32[768,256]{1,0:T(8,128)}, f32[768,256]{1,0:T(8,128)}, f32[768,256]{1,0:T(8,128)}, f32[768,256]{1,0:T(8,128)}, f32[768,256]{1,0:T(8,128)}, /*i...) custom-call(s32[100]{0:T(128)} %fusion.18.tbl, ...), custom_call_target="tpu_custom_call" | custom-call | flops 1000000000 | bytes 1048576 | tf_op jit(solution)/shard_map/pallas_call | solution.py:189
  330.0 17.6 %collective-permute-start.33 = (bf16[768,512]{1,0:T(8,128)(2,1)S(1)}, bf16[768,512]{1,0:T(8,128)(2,1)S(1)}, u32[]{:S(2)}, u32[]{:S(2)}) collective-permute-start(bf16[768,512]{1,0:T(8,128)(2,1)S(1)} %constant_dynamic-slice_fusion), channel_id=1, source_target_pairs={{0,8},{4,12},{8,0},{12,4},{1,9},{5,13},{9,1},{13,5},{2,10},{6,14},... | collective-permute-start | bytes 2359304 | tf_op jit(solution)/shard_map/ppermute | solution.py:344
  347.6 6.5 %collective-permute-start.32 = (bf16[768,512]{1,0:T(8,128)(2,1)S(1)}, bf16[768,512]{1,0:T(8,128)(2,1)S(1)}, u32[]{:S(2)}, u32[]{:S(2)}) collective-permute-start(bf16[768,512]{1,0:T(8,128)(2,1)S(1)} %constant_dynamic-slice_fusion), channel_id=1, source_target_pairs={{0,4},{4,0},{8,12},{12,8},{1,5},{5,1},{9,13},{13,9},{2,6},{6,2},{1... | collective-permute-start | bytes 2359304 | tf_op jit(solution)/shard_map/ppermute | solution.py:344
  354.1 3.2 collective-permute-start.20
  357.5 51.9 %shard_map.86 = (bf16[768,256]{1,0:T(8,128)(2,1)}, bf16[768,256]{1,0:T(8,128)(2,1)}, bf16[768,256]{1,0:T(8,128)(2,1)}, bf16[768,256]{1,0:T(8,128)(2,1)}) custom-call(s32[100]{0:T(128)} %fusion.17.tbl, bf16[768,768]{1,0:T(8,128)(2,1)} %convolution_convert_fusion.6.refs_0_, bf16[768,768]{1,0:T(8,128)(2,1)} %convolution_convert_fusion.5.refs_1_, ...), custom_call_target="tpu_custom_call" | custom-call | flops 30000001024 | bytes 1048576 | tf_op jit(solution)/shard_map/pallas_call | solution.py:189
  411.9 2.1 constant_dynamic-update-slice_fusion.refs_12_
  415.5 52.4 %shard_map.87 = (bf16[768,256]{1,0:T(8,128)(2,1)}, bf16[768,256]{1,0:T(8,128)(2,1)}, bf16[768,256]{1,0:T(8,128)(2,1)}, bf16[768,256]{1,0:T(8,128)(2,1)}) custom-call(s32[100]{0:T(128)} %fusion.17.tbl, bf16[768,768]{1,0:T(8,128)(2,1)} %convolution_convert_fusion.6.refs_0_, bf16[768,768]{1,0:T(8,128)(2,1)} %convolution_convert_fusion.5.refs_1_, ...), custom_call_target="tpu_custom_call" | custom-call | flops 30000001024 | bytes 1048576 | tf_op jit(solution)/shard_map/pallas_call | solution.py:189
  467.9 52.3 %shard_map.88 = (bf16[768,256]{1,0:T(8,128)(2,1)}, bf16[768,256]{1,0:T(8,128)(2,1)}, bf16[768,256]{1,0:T(8,128)(2,1)}, bf16[768,256]{1,0:T(8,128)(2,1)}) custom-call(s32[100]{0:T(128)} %fusion.17.tbl, bf16[768,768]{1,0:T(8,128)(2,1)} %convolution_convert_fusion.6.refs_0_, bf16[768,768]{1,0:T(8,128)(2,1)} %convolution_convert_fusion.5.refs_1_, ...), custom_call_target="tpu_custom_call" | custom-call | flops 30000001024 | bytes 1048576 | tf_op jit(solution)/shard_map/pallas_call | solution.py:189
  521.9 2.6 collective-permute-start.31
  524.5 7.7 %collective-permute-done.29.refs_9_ = bf16[768,256]{1,0:T(8,128)(2,1)S(1)} collective-permute-done((bf16[768,256]{1,0:T(8,128)(2,1)}, bf16[768,256]{1,0:T(8,128)(2,1)S(1)}, u32[]{:S(2)}, u32[]{:S(2)}) %collective-permute-start.29) | collective-permute-done | bytes 393248 | tf_op jit(solution)/shard_map/ppermute | solution.py:337
  533.4 42.8 %collective-permute-done.31.refs_11_ = bf16[768,256]{1,0:T(8,128)(2,1)S(1)} collective-permute-done((bf16[768,256]{1,0:T(8,128)(2,1)}, bf16[768,256]{1,0:T(8,128)(2,1)S(1)}, u32[]{:S(2)}, u32[]{:S(2)}) %collective-permute-start.31) | collective-permute-done | bytes 393248 | tf_op jit(solution)/shard_map/ppermute | solution.py:337
  576.3 4.7 collective-permute-done.24.refs_6_
  581.0 3.0 collective-permute-start.18
  584.0 25.9 %collective-permute-done.25.refs_7_ = bf16[768,256]{1,0:T(8,128)(2,1)S(1)} collective-permute-done((bf16[768,256]{1,0:T(8,128)(2,1)S(1)}, bf16[768,256]{1,0:T(8,128)(2,1)S(1)}, u32[]{:S(2)}, u32[]{:S(2)}) %collective-permute-start.25) | collective-permute-done | bytes 393248 | tf_op jit(solution)/shard_map/ppermute | solution.py:337
  611.4 3.3 collective-permute-done.18.refs_2_
  614.7 12.2 %collective-permute-done.19.refs_3_ = bf16[768,256]{1,0:T(8,128)(2,1)} collective-permute-done((bf16[768,256]{1,0:T(8,128)(2,1)S(1)}, bf16[768,256]{1,0:T(8,128)(2,1)}, u32[]{:S(2)}, u32[]{:S(2)}) %collective-permute-start.19) | collective-permute-done | bytes 393248 | tf_op jit(solution)/shard_map/ppermute | solution.py:337
  626.9 17.1 %shard_map.89 = bf16[768,2048]{1,0:T(8,128)(2,1)} custom-call(s32[4]{0:T(128)} %pad_add_fusion.tbl, bf16[768,256]{1,0:T(8,128)(2,1)} %get-tuple-element.82.refs_0_, bf16[768,256]{1,0:T(8,128)(2,1)} %collective-permute-done.17.refs_1_, bf16[768,256]{1,0:T(8,128)(2,1)} %collective-permute-done.18.refs_2_, bf16[768,256]{1,0:T(8,128)(2,1)} %collective-permute-done.19.refs_3_, ...), custom_call_target="tpu_custom_call" | custom-call | flops 9663676416 | bytes 16777216 | tf_op jit(solution)/shard_map/pallas_call | solution.py:241
  (93 shorter events, 20.5 us)
Async XLA Ops:
  0.0 193.9 %copy-start = (bf16[6,128,2048]{2,1,0:T(8,128)(2,1)S(1)}, bf16[6,128,2048]{2,1,0:T(8,128)(2,1)}, u32[]{:S(2)}) copy-start(bf16[6,128,2048]{2,1,0:T(8,128)(2,1)} %param.12) | copy-start | bytes 9437188
  0.0 81.2 %collective-permute-start = (bf16[768,2048]{1,0:T(8,128)(2,1)}, bf16[768,2048]{1,0:T(8,128)(2,1)}, u32[]{:S(2)}, u32[]{:S(2)}) collective-permute-start(bf16[768,2048]{1,0:T(8,128)(2,1)} %param.8), channel_id=1, source_target_pairs={{0,4},{4,0},{8,12},{12,8},{1,5},{5,1},{9,13},{13,9},{2,6},{6,2},{1... | collective-permute-start | bytes 9437192 | tf_op jit(solution)/shard_map/ppermute | solution.py:274
  1.3 75.7 %collective-permute-start.3 = (bf16[768,2048]{1,0:T(8,128)(2,1)}, bf16[768,2048]{1,0:T(8,128)(2,1)}, u32[]{:S(2)}, u32[]{:S(2)}) collective-permute-start(bf16[768,2048]{1,0:T(8,128)(2,1)} %param.8), channel_id=1, source_target_pairs={{4,8},{8,4},{5,9},{9,5},{6,10},{10,6},{7,11},{11,7},{20,24},{24,20... | collective-permute-start | bytes 9437192 | tf_op jit(solution)/shard_map/ppermute | solution.py:275
  16.7 66.9 %copy-start.2 = (bf16[2048,6,256]{0,2,1:T(8,128)(2,1)}, bf16[2048,6,256]{0,2,1:T(8,128)(2,1)S(1)}, u32[]{:S(2)}) copy-start(bf16[2048,6,256]{0,2,1:T(8,128)(2,1)S(1)} %pad_maximum_fusion) | copy-start | bytes 18874372
  23.0 52.2 %collective-permute-start.6 = (bf16[768,1536]{1,0:T(8,128)(2,1)}, bf16[768,1536]{1,0:T(8,128)(2,1)}, u32[]{:S(2)}, u32[]{:S(2)}) collective-permute-start(bf16[768,1536]{1,0:T(8,128)(2,1)} %fusion.refs_2_.refs_3_.refs_4_), channel_id=1, source_target_pairs={{0,2},{1,3},{2,0},{3,1},{4,6},{5,7},{6,4},{7,5},{8,10},{9,11},{10,... | collective-permute-start | bytes 7077896 | tf_op jit(solution)/shard_map/ppermute | solution.py:288
  23.2 73.7 %collective-permute-start.5 = (bf16[768,1536]{1,0:T(8,128)(2,1)}, bf16[768,1536]{1,0:T(8,128)(2,1)}, u32[]{:S(2)}, u32[]{:S(2)}) collective-permute-start(bf16[768,1536]{1,0:T(8,128)(2,1)} %fusion.refs_2_.refs_3_.refs_4_), channel_id=1, source_target_pairs={{0,1},{1,0},{2,3},{3,2},{4,5},{5,4},{6,7},{7,6},{8,9},{9,8},{10,11... | collective-permute-start | bytes 7077896 | tf_op jit(solution)/shard_map/ppermute | solution.py:287
  75.1 36.3 %collective-permute-start.7 = (bf16[768,1536]{1,0:T(8,128)(2,1)}, bf16[768,1536]{1,0:T(8,128)(2,1)}, u32[]{:S(2)}, u32[]{:S(2)}) collective-permute-start(bf16[768,1536]{1,0:T(8,128)(2,1)} %collective-permute-done.6.refs_4_.refs_5_.refs_6_), channel_id=1, source_target_pairs={{0,1},{1,0},{2,3},{3,2},{4,5},{5,4},{6,7},{7,6},{8,9},{9,8},{10,11... | collective-permute-start | bytes 7077896 | tf_op jit(solution)/shard_map/ppermute | solution.py:289
  77.0 70.4 %collective-permute-start.4 = (bf16[768,2048]{1,0:T(8,128)(2,1)}, bf16[768,2048]{1,0:T(8,128)(2,1)}, u32[]{:S(2)}, u32[]{:S(2)}) collective-permute-start(bf16[768,2048]{1,0:T(8,128)(2,1)} %collective-permute-done.3), channel_id=1, source_target_pairs={{4,0},{8,12},{5,1},{9,13},{6,2},{10,14},{7,3},{11,15},{20,16},{24,... | collective-permute-start | bytes 9437192 | tf_op jit(solution)/shard_map/ppermute | solution.py:276
  81.2 71.6 %collective-permute-start.1 = (bf16[768,2048]{1,0:T(8,128)(2,1)}, bf16[768,2048]{1,0:T(8,128)(2,1)}, u32[]{:S(2)}, u32[]{:S(2)}) collective-permute-start(bf16[768,2048]{1,0:T(8,128)(2,1)} %collective-permute-done), channel_id=1, source_target_pairs={{4,8},{8,4},{5,9},{9,5},{6,10},{10,6},{7,11},{11,7},{20,24},{24,20... | collective-permute-start | bytes 9437192 | tf_op jit(solution)/shard_map/ppermute | solution.py:277
  91.8 19.7 %collective-permute-start.8 = (bf16[768,1536]{1,0:T(8,128)(2,1)}, bf16[768,1536]{1,0:T(8,128)(2,1)}, u32[]{:S(2)}, u32[]{:S(2)}) collective-permute-start(bf16[768,1536]{1,0:T(8,128)(2,1)} %fusion.1.refs_6_.refs_7_.refs_8_), channel_id=1, source_target_pairs={{0,1},{1,0},{2,3},{3,2},{4,5},{5,4},{6,7},{7,6},{8,9},{9,8},{10,11... | collective-permute-start | bytes 7077896 | tf_op jit(solution)/shard_map/ppermute | solution.py:287
  96.9 73.7 %collective-permute-start.9 = (bf16[768,1536]{1,0:T(8,128)(2,1)}, bf16[768,1536]{1,0:T(8,128)(2,1)}, u32[]{:S(2)}, u32[]{:S(2)}) collective-permute-start(bf16[768,1536]{1,0:T(8,128)(2,1)} %fusion.1.refs_6_.refs_7_.refs_8_), channel_id=1, source_target_pairs={{0,2},{1,3},{2,0},{3,1},{4,6},{5,7},{6,4},{7,5},{8,10},{9,11},{10,... | collective-permute-start | bytes 7077896 | tf_op jit(solution)/shard_map/ppermute | solution.py:288
  152.8 109.1 %collective-permute-start.2 = (bf16[768,2048]{1,0:T(8,128)(2,1)}, bf16[768,2048]{1,0:T(8,128)(2,1)}, u32[]{:S(2)}, u32[]{:S(2)}) collective-permute-start(bf16[768,2048]{1,0:T(8,128)(2,1)} %collective-permute-done.1), channel_id=1, source_target_pairs={{4,0},{8,12},{5,1},{9,13},{6,2},{10,14},{7,3},{11,15},{20,16},{24,... | collective-permute-start | bytes 9437192 | tf_op jit(solution)/shard_map/ppermute | solution.py:278
  165.6 36.5 %collective-permute-start.12 = (bf16[768,1536]{1,0:T(8,128)(2,1)}, bf16[768,1536]{1,0:T(8,128)(2,1)}, u32[]{:S(2)}, u32[]{:S(2)}) collective-permute-start(bf16[768,1536]{1,0:T(8,128)(2,1)} %convolution_convert_fusion.refs_11_.refs_12_), channel_id=1, source_target_pairs={{0,2},{1,3},{2,0},{3,1},{4,6},{5,7},{6,4},{7,5},{8,10},{9,11},{10,... | collective-permute-start | bytes 7077896 | tf_op jit(solution)/shard_map/ppermute | solution.py:288
  170.7 52.5 %collective-permute-start.10 = (bf16[768,1536]{1,0:T(8,128)(2,1)}, bf16[768,1536]{1,0:T(8,128)(2,1)}, u32[]{:S(2)}, u32[]{:S(2)}) collective-permute-start(bf16[768,1536]{1,0:T(8,128)(2,1)} %collective-permute-done.9.refs_9_.refs_10_), channel_id=1, source_target_pairs={{0,1},{1,0},{2,3},{3,2},{4,5},{5,4},{6,7},{7,6},{8,9},{9,8},{10,11... | collective-permute-start | bytes 7077896 | tf_op jit(solution)/shard_map/ppermute | solution.py:289
  191.5 31.7 %collective-permute-start.11 = (bf16[768,1536]{1,0:T(8,128)(2,1)}, bf16[768,1536]{1,0:T(8,128)(2,1)}, u32[]{:S(2)}, u32[]{:S(2)}) collective-permute-start(bf16[768,1536]{1,0:T(8,128)(2,1)} %convolution_convert_fusion.refs_11_.refs_12_), channel_id=1, source_target_pairs={{0,1},{1,0},{2,3},{3,2},{4,5},{5,4},{6,7},{7,6},{8,9},{9,8},{10,11... | collective-permute-start | bytes 7077896 | tf_op jit(solution)/shard_map/ppermute | solution.py:287
  202.1 155.3 %collective-permute-start.13 = (bf16[768,1536]{1,0:T(8,128)(2,1)}, bf16[768,1536]{1,0:T(8,128)(2,1)}, u32[]{:S(2)}, u32[]{:S(2)}) collective-permute-start(bf16[768,1536]{1,0:T(8,128)(2,1)} %collective-permute-done.12.refs_14_), channel_id=1, source_target_pairs={{0,1},{1,0},{2,3},{3,2},{4,5},{5,4},{6,7},{7,6},{8,9},{9,8},{10,11... | collective-permute-start | bytes 7077896 | tf_op jit(solution)/shard_map/ppermute | solution.py:289
  261.9 21.9 %slice-start = ((s8[6291456]{0:T(1024)(128)(4,1)}), s8[2097152]{0:T(1024)(128)(4,1)S(1)}, s32[]{:S(2)}) async-start(s8[6291456]{0:T(1024)(128)(4,1)} %bitcast.37), calls=%async_computation | async-start | bytes 4194304
  268.8 36.5 %collective-permute-start.15 = (bf16[768,512]{1,0:T(8,128)(2,1)}, bf16[768,512]{1,0:T(8,128)(2,1)}, u32[]{:S(2)}, u32[]{:S(2)}) collective-permute-start(bf16[768,512]{1,0:T(8,128)(2,1)} %fusion.8.refs_16_), channel_id=1, source_target_pairs={{0,2},{1,3},{2,0},{3,1},{4,6},{5,7},{6,4},{7,5},{8,10},{9,11},{10,... | collective-permute-start | bytes 2359304 | tf_op jit(solution)/shard_map/ppermute | solution.py:288
  286.5 43.5 %collective-permute-start.14 = (bf16[768,512]{1,0:T(8,128)(2,1)}, bf16[768,512]{1,0:T(8,128)(2,1)}, u32[]{:S(2)}, u32[]{:S(2)}) collective-permute-start(bf16[768,512]{1,0:T(8,128)(2,1)} %fusion.8.refs_16_), channel_id=1, source_target_pairs={{0,1},{1,0},{2,3},{3,2},{4,5},{5,4},{6,7},{7,6},{8,9},{9,8},{10,11... | collective-permute-start | bytes 2359304 | tf_op jit(solution)/shard_map/ppermute | solution.py:287
  286.5 61.1 %collective-permute-start.34 = (bf16[768,512]{1,0:T(8,128)(2,1)S(1)}, bf16[768,512]{1,0:T(8,128)(2,1)}, u32[]{:S(2)}, u32[]{:S(2)}) collective-permute-start(bf16[768,512]{1,0:T(8,128)(2,1)S(1)} %constant_dynamic-slice_fusion), channel_id=1, source_target_pairs={{0,12},{4,8},{8,4},{12,0},{1,13},{5,9},{9,5},{13,1},{2,14},{6,10},... | collective-permute-start | bytes 2359304 | tf_op jit(solution)/shard_map/ppermute | solution.py:344
  303.5 50.6 %collective-permute-start.21 = (bf16[768,512]{1,0:T(8,128)(2,1)}, bf16[768,512]{1,0:T(8,128)(2,1)}, u32[]{:S(2)}, u32[]{:S(2)}) collective-permute-start(bf16[768,512]{1,0:T(8,128)(2,1)} %fusion.11.refs_16_), channel_id=1, source_target_pairs={{0,2},{1,3},{2,0},{3,1},{4,6},{5,7},{6,4},{7,5},{8,10},{9,11},{10,... | collective-permute-start | bytes 2359304 | tf_op jit(solution)/shard_map/ppermute | solution.py:288
  305.3 52.0 %collective-permute-start.16 = (bf16[768,512]{1,0:T(8,128)(2,1)}, bf16[768,512]{1,0:T(8,128)(2,1)}, u32[]{:S(2)}, u32[]{:S(2)}) collective-permute-start(bf16[768,512]{1,0:T(8,128)(2,1)} %collective-permute-done.15.refs_18_), channel_id=1, source_target_pairs={{0,1},{1,0},{2,3},{3,2},{4,5},{5,4},{6,7},{7,6},{8,9},{9,8},{10,11... | collective-permute-start | bytes 2359304 | tf_op jit(solution)/shard_map/ppermute | solution.py:289
  330.0 79.4 %collective-permute-start.33 = (bf16[768,512]{1,0:T(8,128)(2,1)S(1)}, bf16[768,512]{1,0:T(8,128)(2,1)S(1)}, u32[]{:S(2)}, u32[]{:S(2)}) collective-permute-start(bf16[768,512]{1,0:T(8,128)(2,1)S(1)} %constant_dynamic-slice_fusion), channel_id=1, source_target_pairs={{0,8},{4,12},{8,0},{12,4},{1,9},{5,13},{9,1},{13,5},{2,10},{6,14},... | collective-permute-start | bytes 2359304 | tf_op jit(solution)/shard_map/ppermute | solution.py:344
  347.6 62.4 %collective-permute-start.32 = (bf16[768,512]{1,0:T(8,128)(2,1)S(1)}, bf16[768,512]{1,0:T(8,128)(2,1)S(1)}, u32[]{:S(2)}, u32[]{:S(2)}) collective-permute-start(bf16[768,512]{1,0:T(8,128)(2,1)S(1)} %constant_dynamic-slice_fusion), channel_id=1, source_target_pairs={{0,4},{4,0},{8,12},{12,8},{1,5},{5,1},{9,13},{13,9},{2,6},{6,2},{1... | collective-permute-start | bytes 2359304 | tf_op jit(solution)/shard_map/ppermute | solution.py:344
  354.1 61.0 %collective-permute-start.20 = (bf16[768,512]{1,0:T(8,128)(2,1)}, bf16[768,512]{1,0:T(8,128)(2,1)}, u32[]{:S(2)}, u32[]{:S(2)}) collective-permute-start(bf16[768,512]{1,0:T(8,128)(2,1)} %fusion.11.refs_16_), channel_id=1, source_target_pairs={{0,1},{1,0},{2,3},{3,2},{4,5},{5,4},{6,7},{7,6},{8,9},{9,8},{10,11... | collective-permute-start | bytes 2359304 | tf_op jit(solution)/shard_map/ppermute | solution.py:287
  357.3 52.2 %collective-permute-start.27 = (bf16[768,512]{1,0:T(8,128)(2,1)}, bf16[768,512]{1,0:T(8,128)(2,1)}, u32[]{:S(2)}, u32[]{:S(2)}) collective-permute-start(bf16[768,512]{1,0:T(8,128)(2,1)} %fusion.14.refs_16_), channel_id=1, source_target_pairs={{0,2},{1,3},{2,0},{3,1},{4,6},{5,7},{6,4},{7,5},{8,10},{9,11},{10,... | collective-permute-start | bytes 2359304 | tf_op jit(solution)/shard_map/ppermute | solution.py:288
  357.3 58.2 %collective-permute-start.22 = (bf16[768,512]{1,0:T(8,128)(2,1)}, bf16[768,512]{1,0:T(8,128)(2,1)}, u32[]{:S(2)}, u32[]{:S(2)}) collective-permute-start(bf16[768,512]{1,0:T(8,128)(2,1)} %collective-permute-done.21.refs_18_), channel_id=1, source_target_pairs={{0,1},{1,0},{2,3},{3,2},{4,5},{5,4},{6,7},{7,6},{8,9},{9,8},{10,11... | collective-permute-start | bytes 2359304 | tf_op jit(solution)/shard_map/ppermute | solution.py:289
  409.4 58.5 %collective-permute-start.26 = (bf16[768,512]{1,0:T(8,128)(2,1)}, bf16[768,512]{1,0:T(8,128)(2,1)}, u32[]{:S(2)}, u32[]{:S(2)}) collective-permute-start(bf16[768,512]{1,0:T(8,128)(2,1)} %fusion.14.refs_16_), channel_id=1, source_target_pairs={{0,1},{1,0},{2,3},{3,2},{4,5},{5,4},{6,7},{7,6},{8,9},{9,8},{10,11... | collective-permute-start | bytes 2359304 | tf_op jit(solution)/shard_map/ppermute | solution.py:287
  409.5 58.4 %collective-permute-start.28 = (bf16[768,512]{1,0:T(8,128)(2,1)}, bf16[768,512]{1,0:T(8,128)(2,1)}, u32[]{:S(2)}, u32[]{:S(2)}) collective-permute-start(bf16[768,512]{1,0:T(8,128)(2,1)} %collective-permute-done.27.refs_18_), channel_id=1, source_target_pairs={{0,1},{1,0},{2,3},{3,2},{4,5},{5,4},{6,7},{7,6},{8,9},{9,8},{10,11... | collective-permute-start | bytes 2359304 | tf_op jit(solution)/shard_map/ppermute | solution.py:289
  413.9 106.3 %collective-permute-start.35 = (bf16[3072,512]{1,0:T(8,128)(2,1)}, bf16[3072,512]{1,0:T(8,128)(2,1)S(1)}, u32[]{:S(2)}, u32[]{:S(2)}) collective-permute-start(bf16[3072,512]{1,0:T(8,128)(2,1)} %constant_dynamic-update-slice_fusion.refs_12_), channel_id=1, source_target_pairs={{0,16},{16,0},{1,17},{17,1},{2,18},{18,2},{3,19},{19,3},{4,20},{20... | collective-permute-start | bytes 9437192 | tf_op jit(solution)/shard_map/ppermute | solution.py:346
  415.1 211.8 %collective-permute-start.36 = (bf16[3072,512]{1,0:T(8,128)(2,1)}, bf16[3072,512]{1,0:T(8,128)(2,1)}, u32[]{:S(2)}, u32[]{:S(2)}) collective-permute-start(bf16[3072,512]{1,0:T(8,128)(2,1)} %constant_dynamic-update-slice_fusion.refs_12_), channel_id=1, source_target_pairs={{0,1},{1,0},{2,3},{3,2},{4,5},{5,4},{6,7},{7,6},{8,9},{9,8},{10,11... | collective-permute-start | bytes 9437192 | tf_op jit(solution)/shard_map/ppermute | solution.py:347
  467.9 108.3 %copy-start.7 = (bf16[768,256]{1,0:T(8,128)(2,1)S(1)}, bf16[768,256]{1,0:T(8,128)(2,1)}, u32[]{:S(2)}) copy-start(bf16[768,256]{1,0:T(8,128)(2,1)} %get-tuple-element.98) | copy-start | bytes 1179652
  467.9 142.8 %copy-start.6 = (bf16[768,256]{1,0:T(8,128)(2,1)S(1)}, bf16[768,256]{1,0:T(8,128)(2,1)}, u32[]{:S(2)}) copy-start(bf16[768,256]{1,0:T(8,128)(2,1)} %get-tuple-element.85) | copy-start | bytes 1179652
  521.9 105.0 %collective-permute-start.37 = (bf16[3072,512]{1,0:T(8,128)(2,1)S(1)}, bf16[3072,512]{1,0:T(8,128)(2,1)}, u32[]{:S(2)}, u32[]{:S(2)}) collective-permute-start(bf16[3072,512]{1,0:T(8,128)(2,1)S(1)} %collective-permute-done.35.refs_13_), channel_id=1, source_target_pairs={{0,1},{1,0},{2,3},{3,2},{4,5},{5,4},{6,7},{7,6},{8,9},{9,8},{10,11... | collective-permute-start | bytes 9437192 | tf_op jit(solution)/shard_map/ppermute | solution.py:347
  521.9 10.4 %collective-permute-start.29 = (bf16[768,256]{1,0:T(8,128)(2,1)}, bf16[768,256]{1,0:T(8,128)(2,1)S(1)}, u32[]{:S(2)}, u32[]{:S(2)}) collective-permute-start(bf16[768,256]{1,0:T(8,128)(2,1)} %get-tuple-element.109), channel_id=1, source_target_pairs={{0,4},{4,0},{8,12},{12,8},{1,5},{5,1},{9,13},{13,9},{2,6},{6,2},{1... | collective-permute-start | bytes 1179656 | tf_op jit(solution)/shard_map/ppermute | solution.py:337
  521.9 11.2 %collective-permute-start.30 = (bf16[768,256]{1,0:T(8,128)(2,1)}, bf16[768,256]{1,0:T(8,128)(2,1)S(1)}, u32[]{:S(2)}, u32[]{:S(2)}) collective-permute-start(bf16[768,256]{1,0:T(8,128)(2,1)} %get-tuple-element.110), channel_id=1, source_target_pairs={{0,8},{4,12},{8,0},{12,4},{1,9},{5,13},{9,1},{13,5},{2,10},{6,14},... | collective-permute-start | bytes 1179656 | tf_op jit(solution)/shard_map/ppermute | solution.py:337
  521.9 54.3 %collective-permute-start.31 = (bf16[768,256]{1,0:T(8,128)(2,1)}, bf16[768,256]{1,0:T(8,128)(2,1)S(1)}, u32[]{:S(2)}, u32[]{:S(2)}) collective-permute-start(bf16[768,256]{1,0:T(8,128)(2,1)} %get-tuple-element.111), channel_id=1, source_target_pairs={{0,12},{4,8},{8,4},{12,0},{1,13},{5,9},{9,5},{13,1},{2,14},{6,10},... | collective-permute-start | bytes 1179656 | tf_op jit(solution)/shard_map/ppermute | solution.py:337
  532.3 77.7 %copy-start.8 = (bf16[768,256]{1,0:T(8,128)(2,1)}, bf16[768,256]{1,0:T(8,128)(2,1)S(1)}, u32[]{:S(2)}) copy-start(bf16[768,256]{1,0:T(8,128)(2,1)S(1)} %collective-permute-done.29.refs_9_) | copy-start | bytes 1179652
  532.3 44.0 %collective-permute-start.23 = (bf16[768,256]{1,0:T(8,128)(2,1)}, bf16[768,256]{1,0:T(8,128)(2,1)S(1)}, u32[]{:S(2)}, u32[]{:S(2)}) collective-permute-start(bf16[768,256]{1,0:T(8,128)(2,1)} %get-tuple-element.96), channel_id=1, source_target_pairs={{0,4},{4,0},{8,12},{12,8},{1,5},{5,1},{9,13},{13,9},{2,6},{6,2},{1... | collective-permute-start | bytes 1179656 | tf_op jit(solution)/shard_map/ppermute | solution.py:337
  533.1 76.8 %copy-start.9 = (bf16[768,256]{1,0:T(8,128)(2,1)}, bf16[768,256]{1,0:T(8,128)(2,1)S(1)}, u32[]{:S(2)}) copy-start(bf16[768,256]{1,0:T(8,128)(2,1)S(1)} %collective-permute-done.30.refs_10_) | copy-start | bytes 1179652
  533.1 47.9 %collective-permute-start.24 = (bf16[768,256]{1,0:T(8,128)(2,1)}, bf16[768,256]{1,0:T(8,128)(2,1)S(1)}, u32[]{:S(2)}, u32[]{:S(2)}) collective-permute-start(bf16[768,256]{1,0:T(8,128)(2,1)} %get-tuple-element.97), channel_id=1, source_target_pairs={{0,8},{4,12},{8,0},{12,4},{1,9},{5,13},{9,1},{13,5},{2,10},{6,14},... | collective-permute-start | bytes 1179656 | tf_op jit(solution)/shard_map/ppermute | solution.py:337
  576.2 33.8 %copy-start.10 = (bf16[768,256]{1,0:T(8,128)(2,1)}, bf16[768,256]{1,0:T(8,128)(2,1)S(1)}, u32[]{:S(2)}) copy-start(bf16[768,256]{1,0:T(8,128)(2,1)S(1)} %collective-permute-done.31.refs_11_) | copy-start | bytes 1179652
  576.2 33.7 %collective-permute-start.25 = (bf16[768,256]{1,0:T(8,128)(2,1)S(1)}, bf16[768,256]{1,0:T(8,128)(2,1)S(1)}, u32[]{:S(2)}, u32[]{:S(2)}) collective-permute-start(bf16[768,256]{1,0:T(8,128)(2,1)S(1)} %copy-done.7), channel_id=1, source_target_pairs={{0,12},{4,8},{8,4},{12,0},{1,13},{5,9},{9,5},{13,1},{2,14},{6,10},... | collective-permute-start | bytes 1179656 | tf_op jit(solution)/shard_map/ppermute | solution.py:337
  576.2 33.7 %copy-start.11 = (bf16[768,256]{1,0:T(8,128)(2,1)}, bf16[768,256]{1,0:T(8,128)(2,1)S(1)}, u32[]{:S(2)}) copy-start(bf16[768,256]{1,0:T(8,128)(2,1)S(1)} %collective-permute-done.23.refs_5_) | copy-start | bytes 1179652
  576.2 35.2 %collective-permute-start.17 = (bf16[768,256]{1,0:T(8,128)(2,1)}, bf16[768,256]{1,0:T(8,128)(2,1)}, u32[]{:S(2)}, u32[]{:S(2)}) collective-permute-start(bf16[768,256]{1,0:T(8,128)(2,1)} %get-tuple-element.83), channel_id=1, source_target_pairs={{0,4},{4,0},{8,12},{12,8},{1,5},{5,1},{9,13},{13,9},{2,6},{6,2},{1... | collective-permute-start | bytes 1179656 | tf_op jit(solution)/shard_map/ppermute | solution.py:337
  581.0 29.0 %copy-start.12 = (bf16[768,256]{1,0:T(8,128)(2,1)}, bf16[768,256]{1,0:T(8,128)(2,1)S(1)}, u32[]{:S(2)}) copy-start(bf16[768,256]{1,0:T(8,128)(2,1)S(1)} %collective-permute-done.24.refs_6_) | copy-start | bytes 1179652
  581.0 33.7 %collective-permute-start.18 = (bf16[768,256]{1,0:T(8,128)(2,1)}, bf16[768,256]{1,0:T(8,128)(2,1)}, u32[]{:S(2)}, u32[]{:S(2)}) collective-permute-start(bf16[768,256]{1,0:T(8,128)(2,1)} %get-tuple-element.84), channel_id=1, source_target_pairs={{0,8},{4,12},{8,0},{12,4},{1,9},{5,13},{9,1},{13,5},{2,10},{6,14},... | collective-permute-start | bytes 1179656 | tf_op jit(solution)/shard_map/ppermute | solution.py:337
  610.7 16.2 %collective-permute-start.19 = (bf16[768,256]{1,0:T(8,128)(2,1)S(1)}, bf16[768,256]{1,0:T(8,128)(2,1)}, u32[]{:S(2)}, u32[]{:S(2)}) collective-permute-start(bf16[768,256]{1,0:T(8,128)(2,1)S(1)} %copy-done.6), channel_id=1, source_target_pairs={{0,12},{4,8},{8,4},{12,0},{1,13},{5,9},{9,5},{13,1},{2,14},{6,10},... | collective-permute-start | bytes 1179656 | tf_op jit(solution)/shard_map/ppermute | solution.py:337
  (6 other events, 62.5 us)

commit v2 on v1

--- a/solution.py
+++ b/solution.py
@@ -317,16 +317,18 @@
         def attend_second(g, tbl):
             second[g] = attend(tbl, q_steps[:3], pick(0, AVAIL[1]), AVAIL[1], first, 0, (g * per, per), False, hd, 10 ** 9)
 
-        for g in range(GROUPS - 1):
-            attend_second(g, tables[1])
-        x_last = jnp.where(ends, tie(far_out, *[s[0][2] for s in second[:-1]]), far_mid)
+        attend_second(0, tables[1])
+        x_last = jnp.where(ends, tie(far_out, second[0][0][2]), far_mid)
         kv_last, own_last = [], []
         for g in range(GROUPS):
             kv = project(x_last, wkv[:, spans(g)])
             own_last.append(kv)
             kv_last.append({12 + src: (a, g * per) for src, a in enumerate(spread(kv))})
         q_steps.append(project(x_last, wq))
-        attend_second(GROUPS - 1, tie(tables[1], *own_last, q_steps[3]))
+        behind = [*own_last, q_steps[3]]
+        for g in range(1, GROUPS):
+            attend_second(g, tie(tables[1], *behind))
+            behind = [second[g][0][2]]
 
         o_groups = []
         after = second[-1][0][2]

time: 648 us -> 649 us (level)
    ppermute x6, starting transfers between devices: 22.3 us -> 15.4 us  [spread(): chip = lax.ppermute(kv, 'cp', flip('cp', 2))]
  transfers between devices with their start and end apart: 38 -> 38, of which waited for: 11 -> 12; matrix products, arithmetic and copies ran while one was open for 13% -> 13% of each run, Pallas kernels for 37% -> 37%
where the time goes in v2:
time: 649 us; the launch traced here: 645 us
  Pallas kernels  257 us (40%)
  waiting for transfers between devices  167 us (26%)
  starting transfers between devices  131 us (20%)
  matrix products  57.1 us (9%)
  local copies, waits for them, and re-layouts  25 us (4%)
  other arithmetic  7.07 us (1%)
    pallas_call x7, Pallas kernels, attend(): pl.pallas_call(functools.partial(attend_kernel, cfg), grid_spec=pltpu.Pre...  240 us
    ppermute x9, waiting for transfers between devices, device_fn(): lax.ppermute(o_send[j], 'tp', flip('tp', j))  97.3 us
    dot_general x10, matrix products, project(): jnp.dot(xs, w, preferred_element_type=jnp.float32).astype(jnp.bfloat16)  57.1 us
    ppermute x6, waiting for transfers between devices, spread(): chip = lax.ppermute(kv, 'cp', flip('cp', 2))  53.4 us
    ppermute x6, starting transfers between devices, spread(): both = lax.ppermute(chip, 'cp', flip('cp', 1))  44.5 us
    ppermute x3, starting transfers between devices, device_fn(): w_got = [lax.ppermute(w_part, 'tp', flip('tp', j)) for j in range(1, 4)]  42.7 us
    unnamed x38, local copies, waits for them, and re-layouts  19.2 us
    pallas_call x1, Pallas kernels, project_out(): pl.pallas_call(functools.partial(out_kernel, len(o_groups), n_parts), in_...  17.1 us
  transfers between devices with their start and end apart: 38, of which 12 were waited for; matrix products, arithmetic and copies ran while one was open for 13% of the time, Pallas kernels for 37%

profile of v2, /device:TPU:21, one launch (start us, length us, event | category | flops | bytes accessed | tf_op | source)
XLA Modules:
  0.0 644.7 jit_solution(4996336935243705683)
XLA Ops:
  1.3 1.9 collective-permute-start.3
  3.2 4.7 copy.12
  7.9 4.6 copy.13
  12.6 4.1 pad_maximum_fusion
  16.7 6.3 fusion.refs_2_.refs_3_.refs_4_
  24.5 50.7 %collective-permute-done.6.refs_4_.refs_5_.refs_6_ = bf16[768,1536]{1,0:T(8,128)(2,1)} collective-permute-done((bf16[768,1536]{1,0:T(8,128)(2,1)}, bf16[768,1536]{1,0:T(8,128)(2,1)}, u32[]{:S(2)}, u32[]{:S(2)}) %collective-permute-start.6) | collective-permute-done | bytes 2359328 | tf_op jit(solution)/shard_map/ppermute | solution.py:288
  75.2 1.8 collective-permute-start.7
  77.0 4.2 collective-permute-start.4
  81.2 2.2 collective-permute-start.1
  83.5 8.3 %fusion.1.refs_6_.refs_7_.refs_8_ = bf16[768,1536]{1,0:T(8,128)(2,1)} fusion(bf16[2048,1536]{0,1:T(8,128)(2,1)S(1)} %bitcast.34, bf16[768,2048]{1,0:T(8,128)(2,1)} %collective-permute-done), kind=kOutput, calls=%fused_computation.7 | convolution fusion | flops 4833017856 | bytes 11796480 | tf_op jit(solution)/shard_map/dot_general | solution.py:284
  92.2 4.6 copy.11
  97.0 6.5 %convolution_convert_fusion.6.refs_0_ = bf16[768,768]{1,0:T(8,128)(2,1)} fusion(bf16[768,2048]{1,0:T(8,128)(2,1)} %param.8, bf16[2048,768]{0,1:T(8,128)(2,1)} %bitcast.41), kind=kOutput, calls=%fused_computation.17 | convolution fusion | flops 2416508928 | bytes 7471104 | tf_op jit(solution)/shard_map/dot_general | solution.py:284
  104.9 6.5 %convolution_convert_fusion.5.refs_1_ = bf16[768,768]{1,0:T(8,128)(2,1)} fusion(bf16[768,2048]{1,0:T(8,128)(2,1)} %collective-permute-done, bf16[2048,768]{0,1:T(8,128)(2,1)} %bitcast.42), kind=kOutput, calls=%fused_computation.16 | convolution fusion | flops 2416508928 | bytes 7471104 | tf_op jit(solution)/shard_map/dot_general | solution.py:284
  111.4 24.9 %shard_map.82 = (f32[768,768]{1,0:T(8,128)}, f32[768,768]{1,0:T(8,128)}, f32[768,768]{1,0:T(8,128)}, f32[768,768]{1,0:T(8,128)}, f32[768,768]{1,0:T(8,128)}, /*index=5*/f32[768,768]{1,0:T(8,128)}) custom-call(s32[100]{0:T(128)} %fusion.19.tbl, bf16[768,768]{1,0:T(8,128)(2,1)} %convolution_convert_fusion.6.refs_0_, ...), custom_call_target="tpu_custom_call" | custom-call | flops 1000000000 | bytes 1048576 | tf_op jit(solution)/shard_map/pallas_call | solution.py:189
  136.3 11.0 %collective-permute-done.4 = bf16[768,2048]{1,0:T(8,128)(2,1)} collective-permute-done((bf16[768,2048]{1,0:T(8,128)(2,1)}, bf16[768,2048]{1,0:T(8,128)(2,1)}, u32[]{:S(2)}, u32[]{:S(2)}) %collective-permute-start.4) | collective-permute-done | bytes 3145760 | tf_op jit(solution)/shard_map/ppermute | solution.py:276
  147.3 5.5 collective-permute-done.1
  152.8 3.2 collective-permute-start.2
  156.0 9.3 %convolution_convert_fusion.refs_11_.refs_12_ = bf16[768,1536]{1,0:T(8,128)(2,1)} fusion(bf16[2048,1536]{0,1:T(8,128)(2,1)} %bitcast.35, bf16[768,2048]{1,0:T(8,128)(2,1)} %collective-permute-done.4, bf16[768,2048]{1,0:T(8,128)(2,1)} %collective-permute-done.3, pred[]{:T(512)S(6)} %or.3), kind=kOutput, calls=%fused_computation.1 | convolution fusion | flops 4834590720 | bytes 14942209 | tf_op jit(solution)/shard_map/dot_general | solution.py:284
  165.3 5.0 collective-permute-start.12
  170.3 20.9 %collective-permute-start.10 = (bf16[768,1536]{1,0:T(8,128)(2,1)}, bf16[768,1536]{1,0:T(8,128)(2,1)}, u32[]{:S(2)}, u32[]{:S(2)}) collective-permute-start(bf16[768,1536]{1,0:T(8,128)(2,1)} %collective-permute-done.9.refs_9_.refs_10_), channel_id=1, source_target_pairs={{0,1},{1,0},{2,3},{3,2},{4,5},{5,4},{6,7},{7,6},{8,9},{9,8},{10,11... | collective-permute-start | bytes 7077896 | tf_op jit(solution)/shard_map/ppermute | solution.py:289
  193.7 6.6 %convolution_convert_fusion.4.refs_2_ = bf16[768,768]{1,0:T(8,128)(2,1)} fusion(bf16[2048,768]{0,1:T(8,128)(2,1)} %bitcast.43, bf16[768,2048]{1,0:T(8,128)(2,1)} %collective-permute-done.4, bf16[768,2048]{1,0:T(8,128)(2,1)} %collective-permute-done.3, pred[]{:T(512)S(6)} %or.3), kind=kOutput, calls=%fused_computation.15 | convolution fusion | flops 2418081792 | bytes 10616833 | tf_op jit(solution)/shard_map/dot_general | solution.py:284
  201.6 21.2 %collective-permute-start.13 = (bf16[768,1536]{1,0:T(8,128)(2,1)}, bf16[768,1536]{1,0:T(8,128)(2,1)}, u32[]{:S(2)}, u32[]{:S(2)}) collective-permute-start(bf16[768,1536]{1,0:T(8,128)(2,1)} %collective-permute-done.12.refs_14_), channel_id=1, source_target_pairs={{0,1},{1,0},{2,3},{3,2},{4,5},{5,4},{6,7},{7,6},{8,9},{9,8},{10,11... | collective-permute-start | bytes 7077896 | tf_op jit(solution)/shard_map/ppermute | solution.py:289
  222.8 19.6 %shard_map.83 = (f32[768,256]{1,0:T(8,128)}, f32[768,256]{1,0:T(8,128)}, f32[768,256]{1,0:T(8,128)}, f32[768,256]{1,0:T(8,128)}, f32[768,256]{1,0:T(8,128)}, /*i...) custom-call(s32[100]{0:T(128)} %fusion.18.tbl, ...), custom_call_target="tpu_custom_call" | custom-call | flops 1000000000 | bytes 1048576 | tf_op jit(solution)/shard_map/pallas_call | solution.py:189
  242.4 2.4 broadcast_select_fusion
  244.8 4.5 fusion.8.refs_16_
  249.3 8.2 %collective-permute-start.15 = (bf16[768,512]{1,0:T(8,128)(2,1)}, bf16[768,512]{1,0:T(8,128)(2,1)}, u32[]{:S(2)}, u32[]{:S(2)}) collective-permute-start(bf16[768,512]{1,0:T(8,128)(2,1)} %fusion.8.refs_16_), channel_id=1, source_target_pairs={{0,2},{1,3},{2,0},{3,1},{4,6},{5,7},{6,4},{7,5},{8,10},{9,11},{10,... | collective-permute-start | bytes 2359304 | tf_op jit(solution)/shard_map/ppermute | solution.py:288
  257.5 2.7 fusion.14.refs_16_
  260.3 7.5 %collective-permute-start.34 = (bf16[768,512]{1,0:T(8,128)(2,1)S(1)}, bf16[768,512]{1,0:T(8,128)(2,1)}, u32[]{:S(2)}, u32[]{:S(2)}) collective-permute-start(bf16[768,512]{1,0:T(8,128)(2,1)S(1)} %constant_dynamic-slice_fusion), channel_id=1, source_target_pairs={{0,12},{4,8},{8,4},{12,0},{1,13},{5,9},{9,5},{13,1},{2,14},{6,10},... | collective-permute-start | bytes 2359304 | tf_op jit(solution)/shard_map/ppermute | solution.py:346
  267.8 2.7 fusion.11.refs_16_
  273.5 3.7 convolution_convert_fusion.3.refs_3_
  277.2 19.3 %shard_map.84 = (f32[768,256]{1,0:T(8,128)}, f32[768,256]{1,0:T(8,128)}, f32[768,256]{1,0:T(8,128)}, f32[768,256]{1,0:T(8,128)}, f32[768,256]{1,0:T(8,128)}, /*i...) custom-call(s32[100]{0:T(128)} %fusion.18.tbl, ...), custom_call_target="tpu_custom_call" | custom-call | flops 1000000000 | bytes 1048576 | tf_op jit(solution)/shard_map/pallas_call | solution.py:189
  296.5 19.3 %shard_map.85 = (f32[768,256]{1,0:T(8,128)}, f32[768,256]{1,0:T(8,128)}, f32[768,256]{1,0:T(8,128)}, f32[768,256]{1,0:T(8,128)}, f32[768,256]{1,0:T(8,128)}, /*i...) custom-call(s32[100]{0:T(128)} %fusion.18.tbl, ...), custom_call_target="tpu_custom_call" | custom-call | flops 1000000000 | bytes 1048576 | tf_op jit(solution)/shard_map/pallas_call | solution.py:189
  316.8 28.7 %collective-permute-start.33 = (bf16[768,512]{1,0:T(8,128)(2,1)S(1)}, bf16[768,512]{1,0:T(8,128)(2,1)S(1)}, u32[]{:S(2)}, u32[]{:S(2)}) collective-permute-start(bf16[768,512]{1,0:T(8,128)(2,1)S(1)} %constant_dynamic-slice_fusion), channel_id=1, source_target_pairs={{0,8},{4,12},{8,0},{12,4},{1,9},{5,13},{9,1},{13,5},{2,10},{6,14},... | collective-permute-start | bytes 2359304 | tf_op jit(solution)/shard_map/ppermute | solution.py:346
  345.5 6.5 %collective-permute-start.32 = (bf16[768,512]{1,0:T(8,128)(2,1)S(1)}, bf16[768,512]{1,0:T(8,128)(2,1)S(1)}, u32[]{:S(2)}, u32[]{:S(2)}) collective-permute-start(bf16[768,512]{1,0:T(8,128)(2,1)S(1)} %constant_dynamic-slice_fusion), channel_id=1, source_target_pairs={{0,4},{4,0},{8,12},{12,8},{1,5},{5,1},{9,13},{13,9},{2,6},{6,2},{1... | collective-permute-start | bytes 2359304 | tf_op jit(solution)/shard_map/ppermute | solution.py:346
  352.0 5.8 collective-permute-start.20
  358.0 52.2 %shard_map.86 = (bf16[768,256]{1,0:T(8,128)(2,1)}, bf16[768,256]{1,0:T(8,128)(2,1)}, bf16[768,256]{1,0:T(8,128)(2,1)}, bf16[768,256]{1,0:T(8,128)(2,1)}) custom-call(s32[100]{0:T(128)} %fusion.17.tbl, bf16[768,768]{1,0:T(8,128)(2,1)} %convolution_convert_fusion.6.refs_0_, bf16[768,768]{1,0:T(8,128)(2,1)} %convolution_convert_fusion.5.refs_1_, ...), custom_call_target="tpu_custom_call" | custom-call | flops 30000001024 | bytes 1048576 | tf_op jit(solution)/shard_map/pallas_call | solution.py:189
  412.6 2.1 constant_dynamic-update-slice_fusion.refs_12_
  416.2 52.0 %shard_map.87 = (bf16[768,256]{1,0:T(8,128)(2,1)}, bf16[768,256]{1,0:T(8,128)(2,1)}, bf16[768,256]{1,0:T(8,128)(2,1)}, bf16[768,256]{1,0:T(8,128)(2,1)}) custom-call(s32[100]{0:T(128)} %fusion.17.tbl, bf16[768,768]{1,0:T(8,128)(2,1)} %convolution_convert_fusion.6.refs_0_, bf16[768,768]{1,0:T(8,128)(2,1)} %convolution_convert_fusion.5.refs_1_, ...), custom_call_target="tpu_custom_call" | custom-call | flops 30000001024 | bytes 1048576 | tf_op jit(solution)/shard_map/pallas_call | solution.py:189
  468.2 52.4 %shard_map.88 = (bf16[768,256]{1,0:T(8,128)(2,1)}, bf16[768,256]{1,0:T(8,128)(2,1)}, bf16[768,256]{1,0:T(8,128)(2,1)}, bf16[768,256]{1,0:T(8,128)(2,1)}) custom-call(s32[100]{0:T(128)} %fusion.17.tbl, bf16[768,768]{1,0:T(8,128)(2,1)} %convolution_convert_fusion.6.refs_0_, bf16[768,768]{1,0:T(8,128)(2,1)} %convolution_convert_fusion.5.refs_1_, ...), custom_call_target="tpu_custom_call" | custom-call | flops 30000001024 | bytes 1048576 | tf_op jit(solution)/shard_map/pallas_call | solution.py:189
  522.3 2.6 collective-permute-start.31
  524.9 7.7 %collective-permute-done.29.refs_9_ = bf16[768,256]{1,0:T(8,128)(2,1)S(1)} collective-permute-done((bf16[768,256]{1,0:T(8,128)(2,1)}, bf16[768,256]{1,0:T(8,128)(2,1)S(1)}, u32[]{:S(2)}, u32[]{:S(2)}) %collective-permute-start.29) | collective-permute-done | bytes 393248 | tf_op jit(solution)/shard_map/ppermute | solution.py:339
  533.8 42.8 %collective-permute-done.31.refs_11_ = bf16[768,256]{1,0:T(8,128)(2,1)S(1)} collective-permute-done((bf16[768,256]{1,0:T(8,128)(2,1)}, bf16[768,256]{1,0:T(8,128)(2,1)S(1)}, u32[]{:S(2)}, u32[]{:S(2)}) %collective-permute-start.31) | collective-permute-done | bytes 393248 | tf_op jit(solution)/shard_map/ppermute | solution.py:339
  576.7 4.7 collective-permute-done.24.refs_6_
  581.4 3.0 collective-permute-start.18
  584.4 25.9 %collective-permute-done.25.refs_7_ = bf16[768,256]{1,0:T(8,128)(2,1)S(1)} collective-permute-done((bf16[768,256]{1,0:T(8,128)(2,1)S(1)}, bf16[768,256]{1,0:T(8,128)(2,1)S(1)}, u32[]{:S(2)}, u32[]{:S(2)}) %collective-permute-start.25) | collective-permute-done | bytes 393248 | tf_op jit(solution)/shard_map/ppermute | solution.py:339
  611.7 3.4 collective-permute-done.18.refs_2_
  615.1 12.2 %collective-permute-done.19.refs_3_ = bf16[768,256]{1,0:T(8,128)(2,1)} collective-permute-done((bf16[768,256]{1,0:T(8,128)(2,1)S(1)}, bf16[768,256]{1,0:T(8,128)(2,1)}, u32[]{:S(2)}, u32[]{:S(2)}) %collective-permute-start.19) | collective-permute-done | bytes 393248 | tf_op jit(solution)/shard_map/ppermute | solution.py:339
  627.3 17.1 %shard_map.89 = bf16[768,2048]{1,0:T(8,128)(2,1)} custom-call(s32[4]{0:T(128)} %pad_add_fusion.tbl, bf16[768,256]{1,0:T(8,128)(2,1)} %get-tuple-element.84.refs_0_, bf16[768,256]{1,0:T(8,128)(2,1)} %collective-permute-done.17.refs_1_, bf16[768,256]{1,0:T(8,128)(2,1)} %collective-permute-done.18.refs_2_, bf16[768,256]{1,0:T(8,128)(2,1)} %collective-permute-done.19.refs_3_, ...), custom_call_target="tpu_custom_call" | custom-call | flops 9663676416 | bytes 16777216 | tf_op jit(solution)/shard_map/pallas_call | solution.py:241
  (93 shorter events, 21.0 us)
Async XLA Ops:
  0.0 193.6 %copy-start = (bf16[6,128,2048]{2,1,0:T(8,128)(2,1)S(1)}, bf16[6,128,2048]{2,1,0:T(8,128)(2,1)}, u32[]{:S(2)}) copy-start(bf16[6,128,2048]{2,1,0:T(8,128)(2,1)} %param.12) | copy-start | bytes 9437188
  0.0 81.2 %collective-permute-start = (bf16[768,2048]{1,0:T(8,128)(2,1)}, bf16[768,2048]{1,0:T(8,128)(2,1)}, u32[]{:S(2)}, u32[]{:S(2)}) collective-permute-start(bf16[768,2048]{1,0:T(8,128)(2,1)} %param.8), channel_id=1, source_target_pairs={{0,4},{4,0},{8,12},{12,8},{1,5},{5,1},{9,13},{13,9},{2,6},{6,2},{1... | collective-permute-start | bytes 9437192 | tf_op jit(solution)/shard_map/ppermute | solution.py:274
  1.3 75.7 %collective-permute-start.3 = (bf16[768,2048]{1,0:T(8,128)(2,1)}, bf16[768,2048]{1,0:T(8,128)(2,1)}, u32[]{:S(2)}, u32[]{:S(2)}) collective-permute-start(bf16[768,2048]{1,0:T(8,128)(2,1)} %param.8), channel_id=1, source_target_pairs={{4,8},{8,4},{5,9},{9,5},{6,10},{10,6},{7,11},{11,7},{20,24},{24,20... | collective-permute-start | bytes 9437192 | tf_op jit(solution)/shard_map/ppermute | solution.py:275
  16.7 66.8 %copy-start.2 = (bf16[2048,6,256]{0,2,1:T(8,128)(2,1)}, bf16[2048,6,256]{0,2,1:T(8,128)(2,1)S(1)}, u32[]{:S(2)}) copy-start(bf16[2048,6,256]{0,2,1:T(8,128)(2,1)S(1)} %pad_maximum_fusion) | copy-start | bytes 18874372
  23.0 52.2 %collective-permute-start.6 = (bf16[768,1536]{1,0:T(8,128)(2,1)}, bf16[768,1536]{1,0:T(8,128)(2,1)}, u32[]{:S(2)}, u32[]{:S(2)}) collective-permute-start(bf16[768,1536]{1,0:T(8,128)(2,1)} %fusion.refs_2_.refs_3_.refs_4_), channel_id=1, source_target_pairs={{0,2},{1,3},{2,0},{3,1},{4,6},{5,7},{6,4},{7,5},{8,10},{9,11},{10,... | collective-permute-start | bytes 7077896 | tf_op jit(solution)/shard_map/ppermute | solution.py:288
  23.2 73.6 %collective-permute-start.5 = (bf16[768,1536]{1,0:T(8,128)(2,1)}, bf16[768,1536]{1,0:T(8,128)(2,1)}, u32[]{:S(2)}, u32[]{:S(2)}) collective-permute-start(bf16[768,1536]{1,0:T(8,128)(2,1)} %fusion.refs_2_.refs_3_.refs_4_), channel_id=1, source_target_pairs={{0,1},{1,0},{2,3},{3,2},{4,5},{5,4},{6,7},{7,6},{8,9},{9,8},{10,11... | collective-permute-start | bytes 7077896 | tf_op jit(solution)/shard_map/ppermute | solution.py:287
  75.2 36.2 %collective-permute-start.7 = (bf16[768,1536]{1,0:T(8,128)(2,1)}, bf16[768,1536]{1,0:T(8,128)(2,1)}, u32[]{:S(2)}, u32[]{:S(2)}) collective-permute-start(bf16[768,1536]{1,0:T(8,128)(2,1)} %collective-permute-done.6.refs_4_.refs_5_.refs_6_), channel_id=1, source_target_pairs={{0,1},{1,0},{2,3},{3,2},{4,5},{5,4},{6,7},{7,6},{8,9},{9,8},{10,11... | collective-permute-start | bytes 7077896 | tf_op jit(solution)/shard_map/ppermute | solution.py:289
  77.0 70.3 %collective-permute-start.4 = (bf16[768,2048]{1,0:T(8,128)(2,1)}, bf16[768,2048]{1,0:T(8,128)(2,1)}, u32[]{:S(2)}, u32[]{:S(2)}) collective-permute-start(bf16[768,2048]{1,0:T(8,128)(2,1)} %collective-permute-done.3), channel_id=1, source_target_pairs={{4,0},{8,12},{5,1},{9,13},{6,2},{10,14},{7,3},{11,15},{20,16},{24,... | collective-permute-start | bytes 9437192 | tf_op jit(solution)/shard_map/ppermute | solution.py:276
  81.2 71.6 %collective-permute-start.1 = (bf16[768,2048]{1,0:T(8,128)(2,1)}, bf16[768,2048]{1,0:T(8,128)(2,1)}, u32[]{:S(2)}, u32[]{:S(2)}) collective-permute-start(bf16[768,2048]{1,0:T(8,128)(2,1)} %collective-permute-done), channel_id=1, source_target_pairs={{4,8},{8,4},{5,9},{9,5},{6,10},{10,6},{7,11},{11,7},{20,24},{24,20... | collective-permute-start | bytes 9437192 | tf_op jit(solution)/shard_map/ppermute | solution.py:277
  91.7 19.6 %collective-permute-start.8 = (bf16[768,1536]{1,0:T(8,128)(2,1)}, bf16[768,1536]{1,0:T(8,128)(2,1)}, u32[]{:S(2)}, u32[]{:S(2)}) collective-permute-start(bf16[768,1536]{1,0:T(8,128)(2,1)} %fusion.1.refs_6_.refs_7_.refs_8_), channel_id=1, source_target_pairs={{0,1},{1,0},{2,3},{3,2},{4,5},{5,4},{6,7},{7,6},{8,9},{9,8},{10,11... | collective-permute-start | bytes 7077896 | tf_op jit(solution)/shard_map/ppermute | solution.py:287
  96.8 73.4 %collective-permute-start.9 = (bf16[768,1536]{1,0:T(8,128)(2,1)}, bf16[768,1536]{1,0:T(8,128)(2,1)}, u32[]{:S(2)}, u32[]{:S(2)}) collective-permute-start(bf16[768,1536]{1,0:T(8,128)(2,1)} %fusion.1.refs_6_.refs_7_.refs_8_), channel_id=1, source_target_pairs={{0,2},{1,3},{2,0},{3,1},{4,6},{5,7},{6,4},{7,5},{8,10},{9,11},{10,... | collective-permute-start | bytes 7077896 | tf_op jit(solution)/shard_map/ppermute | solution.py:288
  152.8 89.6 %collective-permute-start.2 = (bf16[768,2048]{1,0:T(8,128)(2,1)}, bf16[768,2048]{1,0:T(8,128)(2,1)}, u32[]{:S(2)}, u32[]{:S(2)}) collective-permute-start(bf16[768,2048]{1,0:T(8,128)(2,1)} %collective-permute-done.1), channel_id=1, source_target_pairs={{4,0},{8,12},{5,1},{9,13},{6,2},{10,14},{7,3},{11,15},{20,16},{24,... | collective-permute-start | bytes 9437192 | tf_op jit(solution)/shard_map/ppermute | solution.py:278
  165.3 36.4 %collective-permute-start.12 = (bf16[768,1536]{1,0:T(8,128)(2,1)}, bf16[768,1536]{1,0:T(8,128)(2,1)}, u32[]{:S(2)}, u32[]{:S(2)}) collective-permute-start(bf16[768,1536]{1,0:T(8,128)(2,1)} %convolution_convert_fusion.refs_11_.refs_12_), channel_id=1, source_target_pairs={{0,2},{1,3},{2,0},{3,1},{4,6},{5,7},{6,4},{7,5},{8,10},{9,11},{10,... | collective-permute-start | bytes 7077896 | tf_op jit(solution)/shard_map/ppermute | solution.py:288
  170.3 52.5 %collective-permute-start.10 = (bf16[768,1536]{1,0:T(8,128)(2,1)}, bf16[768,1536]{1,0:T(8,128)(2,1)}, u32[]{:S(2)}, u32[]{:S(2)}) collective-permute-start(bf16[768,1536]{1,0:T(8,128)(2,1)} %collective-permute-done.9.refs_9_.refs_10_), channel_id=1, source_target_pairs={{0,1},{1,0},{2,3},{3,2},{4,5},{5,4},{6,7},{7,6},{8,9},{9,8},{10,11... | collective-permute-start | bytes 7077896 | tf_op jit(solution)/shard_map/ppermute | solution.py:289
  191.1 31.7 %collective-permute-start.11 = (bf16[768,1536]{1,0:T(8,128)(2,1)}, bf16[768,1536]{1,0:T(8,128)(2,1)}, u32[]{:S(2)}, u32[]{:S(2)}) collective-permute-start(bf16[768,1536]{1,0:T(8,128)(2,1)} %convolution_convert_fusion.refs_11_.refs_12_), channel_id=1, source_target_pairs={{0,1},{1,0},{2,3},{3,2},{4,5},{5,4},{6,7},{7,6},{8,9},{9,8},{10,11... | collective-permute-start | bytes 7077896 | tf_op jit(solution)/shard_map/ppermute | solution.py:287
  201.6 156.2 %collective-permute-start.13 = (bf16[768,1536]{1,0:T(8,128)(2,1)}, bf16[768,1536]{1,0:T(8,128)(2,1)}, u32[]{:S(2)}, u32[]{:S(2)}) collective-permute-start(bf16[768,1536]{1,0:T(8,128)(2,1)} %collective-permute-done.12.refs_14_), channel_id=1, source_target_pairs={{0,1},{1,0},{2,3},{3,2},{4,5},{5,4},{6,7},{7,6},{8,9},{9,8},{10,11... | collective-permute-start | bytes 7077896 | tf_op jit(solution)/shard_map/ppermute | solution.py:289
  249.3 24.2 %collective-permute-start.15 = (bf16[768,512]{1,0:T(8,128)(2,1)}, bf16[768,512]{1,0:T(8,128)(2,1)}, u32[]{:S(2)}, u32[]{:S(2)}) collective-permute-start(bf16[768,512]{1,0:T(8,128)(2,1)} %fusion.8.refs_16_), channel_id=1, source_target_pairs={{0,2},{1,3},{2,0},{3,1},{4,6},{5,7},{6,4},{7,5},{8,10},{9,11},{10,... | collective-permute-start | bytes 2359304 | tf_op jit(solution)/shard_map/ppermute | solution.py:288
  260.3 56.5 %collective-permute-start.14 = (bf16[768,512]{1,0:T(8,128)(2,1)}, bf16[768,512]{1,0:T(8,128)(2,1)}, u32[]{:S(2)}, u32[]{:S(2)}) collective-permute-start(bf16[768,512]{1,0:T(8,128)(2,1)} %fusion.8.refs_16_), channel_id=1, source_target_pairs={{0,1},{1,0},{2,3},{3,2},{4,5},{5,4},{6,7},{7,6},{8,9},{9,8},{10,11... | collective-permute-start | bytes 2359304 | tf_op jit(solution)/shard_map/ppermute | solution.py:287
  260.3 85.2 %collective-permute-start.34 = (bf16[768,512]{1,0:T(8,128)(2,1)S(1)}, bf16[768,512]{1,0:T(8,128)(2,1)}, u32[]{:S(2)}, u32[]{:S(2)}) collective-permute-start(bf16[768,512]{1,0:T(8,128)(2,1)S(1)} %constant_dynamic-slice_fusion), channel_id=1, source_target_pairs={{0,12},{4,8},{8,4},{12,0},{1,13},{5,9},{9,5},{13,1},{2,14},{6,10},... | collective-permute-start | bytes 2359304 | tf_op jit(solution)/shard_map/ppermute | solution.py:346
  270.5 81.5 %collective-permute-start.21 = (bf16[768,512]{1,0:T(8,128)(2,1)}, bf16[768,512]{1,0:T(8,128)(2,1)}, u32[]{:S(2)}, u32[]{:S(2)}) collective-permute-start(bf16[768,512]{1,0:T(8,128)(2,1)} %fusion.11.refs_16_), channel_id=1, source_target_pairs={{0,2},{1,3},{2,0},{3,1},{4,6},{5,7},{6,4},{7,5},{8,10},{9,11},{10,... | collective-permute-start | bytes 2359304 | tf_op jit(solution)/shard_map/ppermute | solution.py:288
  273.5 84.3 %collective-permute-start.16 = (bf16[768,512]{1,0:T(8,128)(2,1)}, bf16[768,512]{1,0:T(8,128)(2,1)}, u32[]{:S(2)}, u32[]{:S(2)}) collective-permute-start(bf16[768,512]{1,0:T(8,128)(2,1)} %collective-permute-done.15.refs_18_), channel_id=1, source_target_pairs={{0,1},{1,0},{2,3},{3,2},{4,5},{5,4},{6,7},{7,6},{8,9},{9,8},{10,11... | collective-permute-start | bytes 2359304 | tf_op jit(solution)/shard_map/ppermute | solution.py:289
  316.8 93.3 %collective-permute-start.33 = (bf16[768,512]{1,0:T(8,128)(2,1)S(1)}, bf16[768,512]{1,0:T(8,128)(2,1)S(1)}, u32[]{:S(2)}, u32[]{:S(2)}) collective-permute-start(bf16[768,512]{1,0:T(8,128)(2,1)S(1)} %constant_dynamic-slice_fusion), channel_id=1, source_target_pairs={{0,8},{4,12},{8,0},{12,4},{1,9},{5,13},{9,1},{13,5},{2,10},{6,14},... | collective-permute-start | bytes 2359304 | tf_op jit(solution)/shard_map/ppermute | solution.py:346
  345.5 65.2 %collective-permute-start.32 = (bf16[768,512]{1,0:T(8,128)(2,1)S(1)}, bf16[768,512]{1,0:T(8,128)(2,1)S(1)}, u32[]{:S(2)}, u32[]{:S(2)}) collective-permute-start(bf16[768,512]{1,0:T(8,128)(2,1)S(1)} %constant_dynamic-slice_fusion), channel_id=1, source_target_pairs={{0,4},{4,0},{8,12},{12,8},{1,5},{5,1},{9,13},{13,9},{2,6},{6,2},{1... | collective-permute-start | bytes 2359304 | tf_op jit(solution)/shard_map/ppermute | solution.py:346
  352.0 63.9 %collective-permute-start.20 = (bf16[768,512]{1,0:T(8,128)(2,1)}, bf16[768,512]{1,0:T(8,128)(2,1)}, u32[]{:S(2)}, u32[]{:S(2)}) collective-permute-start(bf16[768,512]{1,0:T(8,128)(2,1)} %fusion.11.refs_16_), channel_id=1, source_target_pairs={{0,1},{1,0},{2,3},{3,2},{4,5},{5,4},{6,7},{7,6},{8,9},{9,8},{10,11... | collective-permute-start | bytes 2359304 | tf_op jit(solution)/shard_map/ppermute | solution.py:287
  357.8 52.4 %collective-permute-start.27 = (bf16[768,512]{1,0:T(8,128)(2,1)}, bf16[768,512]{1,0:T(8,128)(2,1)}, u32[]{:S(2)}, u32[]{:S(2)}) collective-permute-start(bf16[768,512]{1,0:T(8,128)(2,1)} %fusion.14.refs_16_), channel_id=1, source_target_pairs={{0,2},{1,3},{2,0},{3,1},{4,6},{5,7},{6,4},{7,5},{8,10},{9,11},{10,... | collective-permute-start | bytes 2359304 | tf_op jit(solution)/shard_map/ppermute | solution.py:288
  357.8 58.4 %collective-permute-start.22 = (bf16[768,512]{1,0:T(8,128)(2,1)}, bf16[768,512]{1,0:T(8,128)(2,1)}, u32[]{:S(2)}, u32[]{:S(2)}) collective-permute-start(bf16[768,512]{1,0:T(8,128)(2,1)} %collective-permute-done.21.refs_18_), channel_id=1, source_target_pairs={{0,1},{1,0},{2,3},{3,2},{4,5},{5,4},{6,7},{7,6},{8,9},{9,8},{10,11... | collective-permute-start | bytes 2359304 | tf_op jit(solution)/shard_map/ppermute | solution.py:289
  410.1 58.1 %collective-permute-start.26 = (bf16[768,512]{1,0:T(8,128)(2,1)}, bf16[768,512]{1,0:T(8,128)(2,1)}, u32[]{:S(2)}, u32[]{:S(2)}) collective-permute-start(bf16[768,512]{1,0:T(8,128)(2,1)} %fusion.14.refs_16_), channel_id=1, source_target_pairs={{0,1},{1,0},{2,3},{3,2},{4,5},{5,4},{6,7},{7,6},{8,9},{9,8},{10,11... | collective-permute-start | bytes 2359304 | tf_op jit(solution)/shard_map/ppermute | solution.py:287
  410.2 58.0 %collective-permute-start.28 = (bf16[768,512]{1,0:T(8,128)(2,1)}, bf16[768,512]{1,0:T(8,128)(2,1)}, u32[]{:S(2)}, u32[]{:S(2)}) collective-permute-start(bf16[768,512]{1,0:T(8,128)(2,1)} %collective-permute-done.27.refs_18_), channel_id=1, source_target_pairs={{0,1},{1,0},{2,3},{3,2},{4,5},{5,4},{6,7},{7,6},{8,9},{9,8},{10,11... | collective-permute-start | bytes 2359304 | tf_op jit(solution)/shard_map/ppermute | solution.py:289
  414.6 106.0 %collective-permute-start.35 = (bf16[3072,512]{1,0:T(8,128)(2,1)}, bf16[3072,512]{1,0:T(8,128)(2,1)S(1)}, u32[]{:S(2)}, u32[]{:S(2)}) collective-permute-start(bf16[3072,512]{1,0:T(8,128)(2,1)} %constant_dynamic-update-slice_fusion.refs_12_), channel_id=1, source_target_pairs={{0,16},{16,0},{1,17},{17,1},{2,18},{18,2},{3,19},{19,3},{4,20},{20... | collective-permute-start | bytes 9437192 | tf_op jit(solution)/shard_map/ppermute | solution.py:348
  415.9 211.5 %collective-permute-start.36 = (bf16[3072,512]{1,0:T(8,128)(2,1)}, bf16[3072,512]{1,0:T(8,128)(2,1)}, u32[]{:S(2)}, u32[]{:S(2)}) collective-permute-start(bf16[3072,512]{1,0:T(8,128)(2,1)} %constant_dynamic-update-slice_fusion.refs_12_), channel_id=1, source_target_pairs={{0,1},{1,0},{2,3},{3,2},{4,5},{5,4},{6,7},{7,6},{8,9},{9,8},{10,11... | collective-permute-start | bytes 9437192 | tf_op jit(solution)/shard_map/ppermute | solution.py:349
  468.2 108.4 %copy-start.7 = (bf16[768,256]{1,0:T(8,128)(2,1)S(1)}, bf16[768,256]{1,0:T(8,128)(2,1)}, u32[]{:S(2)}) copy-start(bf16[768,256]{1,0:T(8,128)(2,1)} %get-tuple-element.100) | copy-start | bytes 1179652
  468.2 142.9 %copy-start.6 = (bf16[768,256]{1,0:T(8,128)(2,1)S(1)}, bf16[768,256]{1,0:T(8,128)(2,1)}, u32[]{:S(2)}) copy-start(bf16[768,256]{1,0:T(8,128)(2,1)} %get-tuple-element.87) | copy-start | bytes 1179652
  522.3 105.0 %collective-permute-start.37 = (bf16[3072,512]{1,0:T(8,128)(2,1)S(1)}, bf16[3072,512]{1,0:T(8,128)(2,1)}, u32[]{:S(2)}, u32[]{:S(2)}) collective-permute-start(bf16[3072,512]{1,0:T(8,128)(2,1)S(1)} %collective-permute-done.35.refs_13_), channel_id=1, source_target_pairs={{0,1},{1,0},{2,3},{3,2},{4,5},{5,4},{6,7},{7,6},{8,9},{9,8},{10,11... | collective-permute-start | bytes 9437192 | tf_op jit(solution)/shard_map/ppermute | solution.py:349
  522.3 10.4 %collective-permute-start.29 = (bf16[768,256]{1,0:T(8,128)(2,1)}, bf16[768,256]{1,0:T(8,128)(2,1)S(1)}, u32[]{:S(2)}, u32[]{:S(2)}) collective-permute-start(bf16[768,256]{1,0:T(8,128)(2,1)} %get-tuple-element.111), channel_id=1, source_target_pairs={{0,4},{4,0},{8,12},{12,8},{1,5},{5,1},{9,13},{13,9},{2,6},{6,2},{1... | collective-permute-start | bytes 1179656 | tf_op jit(solution)/shard_map/ppermute | solution.py:339
  522.3 11.2 %collective-permute-start.30 = (bf16[768,256]{1,0:T(8,128)(2,1)}, bf16[768,256]{1,0:T(8,128)(2,1)S(1)}, u32[]{:S(2)}, u32[]{:S(2)}) collective-permute-start(bf16[768,256]{1,0:T(8,128)(2,1)} %get-tuple-element.112), channel_id=1, source_target_pairs={{0,8},{4,12},{8,0},{12,4},{1,9},{5,13},{9,1},{13,5},{2,10},{6,14},... | collective-permute-start | bytes 1179656 | tf_op jit(solution)/shard_map/ppermute | solution.py:339
  522.3 54.3 %collective-permute-start.31 = (bf16[768,256]{1,0:T(8,128)(2,1)}, bf16[768,256]{1,0:T(8,128)(2,1)S(1)}, u32[]{:S(2)}, u32[]{:S(2)}) collective-permute-start(bf16[768,256]{1,0:T(8,128)(2,1)} %get-tuple-element.113), channel_id=1, source_target_pairs={{0,12},{4,8},{8,4},{12,0},{1,13},{5,9},{9,5},{13,1},{2,14},{6,10},... | collective-permute-start | bytes 1179656 | tf_op jit(solution)/shard_map/ppermute | solution.py:339
  532.7 77.7 %copy-start.8 = (bf16[768,256]{1,0:T(8,128)(2,1)}, bf16[768,256]{1,0:T(8,128)(2,1)S(1)}, u32[]{:S(2)}) copy-start(bf16[768,256]{1,0:T(8,128)(2,1)S(1)} %collective-permute-done.29.refs_9_) | copy-start | bytes 1179652
  532.7 44.0 %collective-permute-start.23 = (bf16[768,256]{1,0:T(8,128)(2,1)}, bf16[768,256]{1,0:T(8,128)(2,1)S(1)}, u32[]{:S(2)}, u32[]{:S(2)}) collective-permute-start(bf16[768,256]{1,0:T(8,128)(2,1)} %get-tuple-element.98), channel_id=1, source_target_pairs={{0,4},{4,0},{8,12},{12,8},{1,5},{5,1},{9,13},{13,9},{2,6},{6,2},{1... | collective-permute-start | bytes 1179656 | tf_op jit(solution)/shard_map/ppermute | solution.py:339
  533.5 76.8 %copy-start.9 = (bf16[768,256]{1,0:T(8,128)(2,1)}, bf16[768,256]{1,0:T(8,128)(2,1)S(1)}, u32[]{:S(2)}) copy-start(bf16[768,256]{1,0:T(8,128)(2,1)S(1)} %collective-permute-done.30.refs_10_) | copy-start | bytes 1179652
  533.5 47.9 %collective-permute-start.24 = (bf16[768,256]{1,0:T(8,128)(2,1)}, bf16[768,256]{1,0:T(8,128)(2,1)S(1)}, u32[]{:S(2)}, u32[]{:S(2)}) collective-permute-start(bf16[768,256]{1,0:T(8,128)(2,1)} %get-tuple-element.99), channel_id=1, source_target_pairs={{0,8},{4,12},{8,0},{12,4},{1,9},{5,13},{9,1},{13,5},{2,10},{6,14},... | collective-permute-start | bytes 1179656 | tf_op jit(solution)/shard_map/ppermute | solution.py:339
  576.6 33.8 %copy-start.10 = (bf16[768,256]{1,0:T(8,128)(2,1)}, bf16[768,256]{1,0:T(8,128)(2,1)S(1)}, u32[]{:S(2)}) copy-start(bf16[768,256]{1,0:T(8,128)(2,1)S(1)} %collective-permute-done.31.refs_11_) | copy-start | bytes 1179652
  576.6 33.7 %collective-permute-start.25 = (bf16[768,256]{1,0:T(8,128)(2,1)S(1)}, bf16[768,256]{1,0:T(8,128)(2,1)S(1)}, u32[]{:S(2)}, u32[]{:S(2)}) collective-permute-start(bf16[768,256]{1,0:T(8,128)(2,1)S(1)} %copy-done.7), channel_id=1, source_target_pairs={{0,12},{4,8},{8,4},{12,0},{1,13},{5,9},{9,5},{13,1},{2,14},{6,10},... | collective-permute-start | bytes 1179656 | tf_op jit(solution)/shard_map/ppermute | solution.py:339
  576.6 33.7 %copy-start.11 = (bf16[768,256]{1,0:T(8,128)(2,1)}, bf16[768,256]{1,0:T(8,128)(2,1)S(1)}, u32[]{:S(2)}) copy-start(bf16[768,256]{1,0:T(8,128)(2,1)S(1)} %collective-permute-done.23.refs_5_) | copy-start | bytes 1179652
  576.7 35.1 %collective-permute-start.17 = (bf16[768,256]{1,0:T(8,128)(2,1)}, bf16[768,256]{1,0:T(8,128)(2,1)}, u32[]{:S(2)}, u32[]{:S(2)}) collective-permute-start(bf16[768,256]{1,0:T(8,128)(2,1)} %get-tuple-element.85), channel_id=1, source_target_pairs={{0,4},{4,0},{8,12},{12,8},{1,5},{5,1},{9,13},{13,9},{2,6},{6,2},{1... | collective-permute-start | bytes 1179656 | tf_op jit(solution)/shard_map/ppermute | solution.py:339
  581.4 29.0 %copy-start.12 = (bf16[768,256]{1,0:T(8,128)(2,1)}, bf16[768,256]{1,0:T(8,128)(2,1)S(1)}, u32[]{:S(2)}) copy-start(bf16[768,256]{1,0:T(8,128)(2,1)S(1)} %collective-permute-done.24.refs_6_) | copy-start | bytes 1179652
  581.4 33.7 %collective-permute-start.18 = (bf16[768,256]{1,0:T(8,128)(2,1)}, bf16[768,256]{1,0:T(8,128)(2,1)}, u32[]{:S(2)}, u32[]{:S(2)}) collective-permute-start(bf16[768,256]{1,0:T(8,128)(2,1)} %get-tuple-element.86), channel_id=1, source_target_pairs={{0,8},{4,12},{8,0},{12,4},{1,9},{5,13},{9,1},{13,5},{2,10},{6,14},... | collective-permute-start | bytes 1179656 | tf_op jit(solution)/shard_map/ppermute | solution.py:339
  611.1 16.2 %collective-permute-start.19 = (bf16[768,256]{1,0:T(8,128)(2,1)S(1)}, bf16[768,256]{1,0:T(8,128)(2,1)}, u32[]{:S(2)}, u32[]{:S(2)}) collective-permute-start(bf16[768,256]{1,0:T(8,128)(2,1)S(1)} %copy-done.6), channel_id=1, source_target_pairs={{0,12},{4,8},{8,4},{12,0},{1,13},{5,9},{9,5},{13,1},{2,14},{6,10},... | collective-permute-start | bytes 1179656 | tf_op jit(solution)/shard_map/ppermute | solution.py:339
  627.3 17.1 %copy-start.1 = (bf16[6,128,2048]{2,1,0:T(8,128)(2,1)S(1)}, bf16[6,128,2048]{2,1,0:T(8,128)(2,1)}, u32[]{:S(2)}) copy-start(bf16[6,128,2048]{2,1,0:T(8,128)(2,1)} %param.12) | copy-start | bytes 9437188
  (6 other events, 47.6 us)
